TPU v7x, 256 devices: a whole 4x4x8 slice. The times are simulated.
256 devices in a mesh: gx: 16 (over x_hi, y, core), gy: 16 (over x_lo, z).
Axes of the slice: x: 4 (x_hi: 2, x_lo: 2; x = x_hi * 2 + x_lo), y: 4, z: 8, core: 2. Of those that a mesh axis runs over, the one named last changes fastest.
Arguments:
- u_old: float32 [3, 512, 512, 256], P(None, 'gx', 'gy'), may hold values from -0.6 to 0.6
- density: float32 [512, 512, 256], P('gx', 'gy'), may hold values from 0.5 to 2
- offsets: float32 [3, 4096, 128], P(None, ('gx', 'gy')), may hold values from 0 to 1
- forces: float32 [3, 4096, 128], P(None, ('gx', 'gy')), may hold values from -60 to 60
- base_x: int32 [4096, 128], P(('gx', 'gy')), may hold values from 0 to 31
- base_y: int32 [4096, 128], P(('gx', 'gy')), may hold values from 0 to 31
- base_z: int32 [4096, 128], P(('gx', 'gy')), may hold values from 0 to 255
- tile_count: int32 [256], P(('gx', 'gy')), may hold values from 1 to 16, as said below
Outputs:
- u_new: float32 [3, 512, 512, 256], P(None, 'gx', 'gy')
- marker_velocity: float32 [3, 4096, 128], P(None, ('gx', 'gy'))
Inputs may be any that keep to these rules, and one draw needn't show every extreme that they name: `tile_count`: every draw has a device with exactly 16 live tiles; loads are skewed, with a mean near a quarter of that.
All inputs are finite; a program needn't handle non-finite values.
Results may differ from a plain program's by a relative error of at most 0.000075.
Values sent between devices are 32-bit elements; how exact they have to be, the bound alone decides.
No kernel may reach another device: no remote copies, remote signals or barrier semaphores. Data moves between devices by JAX's collectives and lax.ppermute only.
A program may use at most 64 MiB of HBM per device.

v0:
```python
import jax
import jax.numpy as jnp
from jax import lax
from jax.experimental import pallas as pl
from jax.experimental.pallas import tpu as pltpu
from jax.sharding import PartitionSpec as P


CX, CY, ROWS, PLANES = 32, 32, 40, 36
GROUPS = 12
WINDOW = 9
REACH = 4
TILES = 16
LIST = 8 * TILES
F32, BF16 = jnp.float32, jnp.bfloat16
VMEM = pl.BlockSpec(memory_space=pltpu.VMEM)
SMEM = pl.BlockSpec(memory_space=pltpu.SMEM)
ANY = pl.BlockSpec(memory_space=pl.ANY)


def stencil(frac):
    root = jnp.sqrt(1.0 + 4.0 * frac - 4.0 * frac * frac)
    return [
        (3.0 - 2.0 * frac - root) / 8.0,
        (3.0 - 2.0 * frac + root) / 8.0,
        (1.0 + 2.0 * frac + root) / 8.0,
        (1.0 + 2.0 * frac - root) / 8.0,
    ]


def spread_four(rows, targets, weights):
    row = lax.broadcasted_iota(jnp.int32, (rows, targets[0].shape[1]), 0)
    total = jnp.zeros(row.shape, F32)
    for target, weight in zip(targets, weights):
        total = jnp.where(row == target, weight, total)
    return total


def split(value):
    high = value.astype(BF16)
    return high, (value - high.astype(F32)).astype(BF16)


def split3(value):
    high, rest = value.astype(BF16), value
    parts = [high]
    for _ in range(2):
        rest = rest - parts[-1].astype(F32)
        parts.append(rest.astype(BF16))
    return parts


def x_table(rows, base_x, first, weights):
    return spread_four(rows, [base_x + (a - first) for a in range(4)], weights)


def y_table(base_y, weights):
    targets = []
    for b in range(4):
        y = base_y + (b - 1)
        targets.append(jnp.where((y < -1) | (y > CY + 1), -1, jnp.where(y < 0, ROWS - 1, y)))
    return spread_four(ROWS, targets, weights)


def one_row(base, target, weights):
    total = jnp.zeros(base.shape, F32)
    for shift, weight in enumerate(weights):
        total = jnp.where(base + (shift - 1) == target, weight, total)
    return total


def z_table(base_z, weights):
    return spread_four(256, [(base_z + c - 1) & 255 for c in range(4)], weights)


def payload_of(pay_ref, off_ref, force_ref, bx_ref, by_ref, bz_ref):
    for t in range(TILES):
        lanes = slice(128 * t, 128 * t + 128)
        for c in range(3):
            pay_ref[c : c + 1, lanes] = off_ref[c, t : t + 1, :]
            pay_ref[3 + c : 4 + c, lanes] = force_ref[c, t : t + 1, :]
        pay_ref[6:7, lanes] = bx_ref[t : t + 1, :].astype(F32)
        pay_ref[7:8, lanes] = by_ref[t : t + 1, :].astype(F32)
        pay_ref[14:15, lanes] = bz_ref[t : t + 1, :].astype(F32)
        pay_ref[15:16, lanes] = jnp.ones((1, 128), F32)
    first, second, third = split3(pay_ref[0:8, :])
    row8 = lax.broadcasted_iota(jnp.int32, first.shape, 0)
    second = jnp.where(row8 < 6, second.astype(F32), pay_ref[8:16, :])
    return jnp.concatenate([first.astype(F32), second, third.astype(F32)], axis=0).astype(BF16)


def columns_of(rows, col_ref):
    columns = jnp.concatenate([rows, jnp.zeros((128 - TILES, 128), F32)], axis=0).T
    for t in range(TILES):
        col_ref[128 * t : 128 * t + 128, :] = jnp.broadcast_to(columns[:, t : t + 1], (128, 128))


def gather(payload, col_ref, j, start, list_ref, base):
    lane = lax.broadcasted_iota(jnp.int32, (128 * TILES, 128), 1).astype(F32)
    here = col_ref[...] - (start + 256 * j).astype(F32)
    pick = jnp.concatenate([jnp.where(here == lane + 128.0 * h, 1.0, 0.0).astype(BF16) for h in range(2)], axis=1)
    parts = jnp.dot(payload, pick, preferred_element_type=F32)
    code = parts[6:7] + 64.0 * parts[7:8] + 4096.0 * parts[14:15]
    row = lax.broadcasted_iota(jnp.int32, (8, 256), 0)
    fields = parts[0:8] + parts[8:16] + parts[16:24]
    fields = jnp.where(row < 6, fields, jnp.where(row == 6, code, 0.0))
    rows = pl.multiple_of(base + 16 * j, 8)
    list_ref[pl.ds(rows, 8), :] = fields[:, :128]
    list_ref[pl.ds(rows + 8, 8), :] = fields[:, 128:]
    return parts


def running():
    i0 = lax.broadcasted_iota(jnp.int32, (128, 256), 0)
    i1 = lax.broadcasted_iota(jnp.int32, (128, 256), 1)
    return jnp.where(i0 <= i1, 1.0, 0.0).astype(BF16)


def scalar(row):
    return jnp.max(row).astype(jnp.int32)


def decode(block):
    weights = [stencil(block[c : c + 1]) for c in range(3)]
    code = block[6:7].astype(jnp.int32)
    return weights, [block[3 + c : 4 + c] for c in range(3)], (code & 63, (code >> 6) & 63, code >> 12)


def pair_of(list_ref, j):
    rows = pl.multiple_of(16 * j, 8)
    return jnp.concatenate([list_ref[pl.ds(rows, 8), :], list_ref[pl.ds(rows + 8, 8), :]], axis=1)


def pack_y_kernel(
    count_ref, off_ref, force_ref, bx_ref, by_ref, bz_ref, u_ref, rho_ref, yn_ref, yp_ref,
    slab, pay_ref, col_ref, sems,
):
    copies = []
    for c in range(4):
        for h in range(2):
            j, lanes = 2 * c + h, pl.ds(128 * h, 128)
            for n in range(2):
                ys = pl.ds((CY - 8) * n, 8)
                src = u_ref.at[c, :, ys, lanes] if c < 3 else rho_ref.at[:, ys, lanes]
                copies.append(pltpu.make_async_copy(src, slab.at[n, j], sems.at[n, j]))
    for copy in copies:
        copy.start()
    count = count_ref[0]
    tile = lax.broadcasted_iota(jnp.int32, (TILES, 128), 0)
    y = jnp.where(tile < count, by_ref[...], CY // 2)
    low, high = (y < 3).astype(F32), (y > CY - 4).astype(F32)
    counts = jnp.dot(jnp.concatenate([low, high], axis=0).astype(BF16), running(), preferred_element_type=F32)
    below = lax.broadcasted_iota(jnp.int32, (2 * TILES, 2 * TILES), 0)
    left = lax.broadcasted_iota(jnp.int32, (2 * TILES, 2 * TILES), 1)
    earlier = jnp.where((left < below) & ((left < TILES) == (below < TILES)), 1.0, 0.0).astype(BF16)
    before = jnp.dot(earlier, counts[:, 128:].astype(BF16), preferred_element_type=F32)
    place = counts[:, :128] + before - 1.0
    columns_of(low * (place[:TILES] + 1.0) + high * (place[TILES:] + 4097.0) - 1.0, col_ref)
    payload = payload_of(pay_ref, off_ref, force_ref, bx_ref, by_ref, bz_ref)
    ends = before + counts[:, 128:]
    for n, (ref, base, start) in enumerate(((yp_ref, 16 * CX, 0), (yn_ref, 8 * CX, 4096))):
        end = ends[TILES * n + TILES - 1 : TILES * n + TILES]
        size = scalar(end)

        def chunk(j, carry, ref=ref, base=base, start=start):
            gather(payload, col_ref, j, start, ref, base)
            return carry

        lax.fori_loop(0, jnp.maximum((size + 255) // 256, 1), chunk, 0)
        ref[base + 7 : base + 8, :] = end
    for copy in copies:
        copy.wait()
    for j in range(8):
        for r in range(2):
            yp_ref[(2 * j + r) * CX : (2 * j + r + 1) * CX, :] = slab[0, j, :, r, :]
        yn_ref[j * CX : (j + 1) * CX, :] = slab[1, j, :, 7, :]


def pack_y(count, arrays, u_old, density):
    return pl.pallas_call(
        pack_y_kernel,
        out_shape=[
            jax.ShapeDtypeStruct((8 * CX + LIST, 128), F32),
            jax.ShapeDtypeStruct((16 * CX + LIST, 128), F32),
        ],
        in_specs=[SMEM] + [VMEM] * 5 + [ANY, ANY],
        out_specs=[VMEM] * 2,
        scratch_shapes=[
            pltpu.VMEM((2, 8, CX, 8, 128), F32),
            pltpu.VMEM((16, 128 * TILES), F32),
            pltpu.VMEM((128 * TILES, 128), F32),
            pltpu.SemaphoreType.DMA((2, 8)),
        ],
        name="pack_y",
    )(count, *arrays, u_old, density)


def sort_kernel(
    count_ref, off_ref, force_ref, bx_ref, by_ref, bz_ref, list_ref, pos_ref, span_ref, pay_ref, col_ref
):
    count = count_ref[0]
    key_row = lax.broadcasted_iota(jnp.int32, (CX, 128), 0)
    keys = [jnp.where(t < count, bx_ref[t : t + 1, :], 2 * CX) for t in range(TILES)]
    same = [(key_row == k).astype(F32) for k in keys]
    less = [(k < key_row).astype(F32) for k in keys]
    counts = jnp.dot(jnp.concatenate(same, axis=0).astype(BF16), running(), preferred_element_type=F32)
    smaller = jnp.dot(sum(less).astype(BF16), jnp.ones((128, 128), BF16), preferred_element_type=F32)
    before = smaller
    for t in range(TILES):
        part = counts[CX * t : CX * t + CX]
        pos_ref[t : t + 1, :] = jnp.sum(same[t] * (part[:, :128] + before), axis=0, keepdims=True) - 1.0
        before = before + part[:, 128:]
    columns_of(pos_ref[...], col_ref)
    payload = payload_of(pay_ref, off_ref, force_ref, bx_ref, by_ref, bz_ref)

    def chunk(j, carry):
        parts = gather(payload, col_ref, j, 0, list_ref, 0)
        there = parts[15:16] > 0.5
        span_ref[2 * j] = jnp.min(jnp.where(there, parts[6:7], 255.0)).astype(jnp.int32)
        span_ref[2 * j + 1] = scalar(jnp.where(there, parts[6:7], 0.0))
        return carry

    lax.fori_loop(0, (count + 1) // 2, chunk, 0)
    list_ref[7:8, :] = smaller[3:4]
    list_ref[15:16, :] = smaller[CX - 3 : CX - 2]
    list_ref[23:24, :] = jnp.full((1, 128), (128 * count).astype(F32))


def sort(count, arrays):
    return pl.pallas_call(
        sort_kernel,
        out_shape=[
            jax.ShapeDtypeStruct((LIST, 128), F32),
            jax.ShapeDtypeStruct((TILES, 128), F32),
            jax.ShapeDtypeStruct((TILES,), jnp.int32),
        ],
        in_specs=[SMEM] + [VMEM] * 5,
        out_specs=[VMEM, VMEM, SMEM],
        scratch_shapes=[pltpu.VMEM((16, 128 * TILES), F32), pltpu.VMEM((128 * TILES, 128), F32)],
        cost_estimate=pl.CostEstimate(flops=3_000_000_000, bytes_accessed=400_000, transcendentals=0),
        name="sort",
    )(count, *arrays)


def pack_x_kernel(u_ref, rho_ref, below_ref, above_ref, list_ref, xn_ref, xp_ref, sems):
    copies = []
    for c in range(4):
        for h in range(2):
            j, lanes = 2 * c + h, pl.ds(128 * h, 128)
            for n, (ref, base, x) in enumerate(
                ((xn_ref, ROWS * j, CX - 1), (xp_ref, 2 * ROWS * j, 0), (xp_ref, 2 * ROWS * j + ROWS, 1))
            ):
                src = u_ref.at[c, x, :, lanes] if c < 3 else rho_ref.at[x, :, lanes]
                copies.append(pltpu.make_async_copy(src, ref.at[pl.ds(base, CY)], sems.at[n, j]))
    for copy in copies:
        copy.start()
    for j in range(8):
        fill = jnp.full((8, 128), 0.0 if j < 6 else 1.0, F32)
        for ref, base, x in (
            (xn_ref, ROWS * j, CX - 1), (xp_ref, 2 * ROWS * j, 0), (xp_ref, 2 * ROWS * j + ROWS, 1)
        ):
            ref[base + CY : base + ROWS, :] = fill
            for r in range(2):
                row = (2 * j + r) * CX + x
                ref[base + CY + r : base + CY + r + 1, :] = above_ref[row : row + 1, :]
            ref[base + ROWS - 1 : base + ROWS, :] = below_ref[j * CX + x : j * CX + x + 1, :]
    for ref, base in ((xn_ref, 8 * ROWS), (xp_ref, 16 * ROWS)):
        ref[base : base + LIST, :] = list_ref[...]
        ref[base + LIST : base + 2 * LIST, :] = below_ref[8 * CX :, :]
        ref[base + 2 * LIST : base + 3 * LIST, :] = above_ref[16 * CX :, :]
    for copy in copies:
        copy.wait()


def pack_x(u_old, density, below, above, markers):
    return pl.pallas_call(
        pack_x_kernel,
        out_shape=[
            jax.ShapeDtypeStruct((8 * ROWS + 3 * LIST, 128), F32),
            jax.ShapeDtypeStruct((16 * ROWS + 3 * LIST, 128), F32),
        ],
        in_specs=[ANY, ANY] + [VMEM] * 3,
        out_specs=[VMEM] * 2,
        scratch_shapes=[pltpu.SemaphoreType.DMA((3, 8))],
        name="pack_x",
    )(u_old, density, below, above, markers)


def spread_list(list_ref, chunks, span_ref, grid_ref, a_ref, b_ref, wx_ref):
    def chunk(j, carry):
        (weight_x, weight_y, weight_z), forces, (base_x, base_y, base_z) = decode(pair_of(list_ref, j))
        wy, wz = y_table(base_y, weight_y), z_table(base_z, weight_z)
        for c in range(3):
            high, low = split(wz * forces[c])
            for part, value in enumerate((high, high, low)):
                b_ref[256 * c : 256 * c + 256, 256 * part : 256 * part + 256] = value
        low_x, high_x = span_ref[2 * j], span_ref[2 * j + 1]

        def window(w, carry):
            first = low_x + WINDOW * w
            wx_ref[...] = x_table(16, base_x, first, weight_x)
            flat = jnp.concatenate([wx_ref[e : e + 1, :] * wy for e in range(WINDOW)], axis=0)
            high, low = split(flat)
            for part, value in enumerate((high, low, high)):
                a_ref[:, 256 * part : 256 * part + 256] = value
            sums = lax.dot_general(
                a_ref[...], b_ref[...], (((1,), (1,)), ((), ())), preferred_element_type=F32
            )
            for j in range(6):
                grid_ref[j, pl.ds(first, WINDOW)] += sums[:, 128 * j : 128 * j + 128].reshape(
                    WINDOW, ROWS, 128
                )
            return carry

        lax.fori_loop(0, (high_x + 4 - low_x + WINDOW - 1) // WINDOW, window, 0)
        return carry

    lax.fori_loop(0, chunks, chunk, 0)


def spread_edge(ref, base, first, last, dx, dy, grid_ref):
    def tile(t, carry):
        rows = pl.ds(pl.multiple_of(base + 8 * t, 8), 8)
        (weight_x, weight_y, weight_z), forces, (base_x, base_y, base_z) = decode(ref[rows, :])
        base_x, base_y = base_x + CX * dx, base_y + CY * dy
        wz = z_table(base_z, weight_z)
        if dx == 0:
            table = x_table(ROWS, base_x, 0, weight_x)
            cells = (-1, 0, 1) if dy < 0 else (CY - 1, CY, CY + 1)
            lines = [one_row(base_y, cell, weight_y) for cell in cells]
        else:
            table = y_table(base_y, weight_y)
            cells = (-1, 0, 1) if dx < 0 else (CX - 1, CX, CX + 1)
            lines = [one_row(base_x, cell, weight_x) for cell in cells]
        a_high, a_low = split(jnp.concatenate([table * line for line in lines], axis=0))
        b_high, b_low = split(jnp.concatenate([wz * force for force in forces], axis=0))
        sums = lax.dot_general(
            jnp.concatenate([a_high, a_low, a_high], axis=1),
            jnp.concatenate([b_high, b_high, b_low], axis=1),
            (((1,), (1,)), ((), ())),
            preferred_element_type=F32,
        )
        for j in range(6):
            part = sums[:, 128 * j : 128 * j + 128]
            if dx == 0:
                for i, cell in enumerate(cells):
                    row = cell % ROWS
                    grid_ref[j, 0:PLANES, row, :] += part[ROWS * i : ROWS * i + PLANES]
            else:
                grid_ref[j, cells[0] + 1 : cells[0] + 4] += part.reshape(3, ROWS, 128)
        return carry

    lax.fori_loop(first, last, tile, 0)


def tiles_of(ref, base):
    return (scalar(ref[base + 7 : base + 8, :]) + 127) // 128


def spread_kernel(count_ref, span_ref, list_ref, below_ref, above_ref, grid_ref, a_ref, b_ref, wx_ref):
    for j in range(6):
        grid_ref[j] = jnp.zeros(grid_ref.shape[1:], F32)
    spread_list(list_ref, (count_ref[0] + 1) // 2, span_ref, grid_ref, a_ref, b_ref, wx_ref)
    spread_edge(below_ref, 8 * CX, 0, tiles_of(below_ref, 8 * CX), 0, -1, grid_ref)
    spread_edge(above_ref, 16 * CX, 0, tiles_of(above_ref, 16 * CX), 0, 1, grid_ref)


def spread(count, span, markers, below, above):
    return pl.pallas_call(
        spread_kernel,
        out_shape=jax.ShapeDtypeStruct((6, PLANES + WINDOW, ROWS, 128), F32),
        in_specs=[SMEM, SMEM] + [VMEM] * 3,
        out_specs=VMEM,
        scratch_shapes=[
            pltpu.VMEM((WINDOW * ROWS, 768), BF16),
            pltpu.VMEM((768, 768), BF16),
            pltpu.VMEM((16, 256), F32),
        ],
        cost_estimate=pl.CostEstimate(flops=6_000_000_000, bytes_accessed=6_000_000, transcendentals=0),
        name="spread",
    )(count, span, markers, below, above)


def finish_kernel(
    count_ref, span_ref, list_ref, pos_ref, u_ref, rho_ref, below_ref, above_ref, left_ref, right_ref, force_ref,
    out_ref, vel_ref, grid_ref, state, ut_ref, a_ref, wx_ref, sorted_ref, sems, out_sem,
):
    count = count_ref[0]
    copies = []
    for c in range(4):
        for h in range(2):
            lanes = pl.ds(128 * h, 128)
            src = u_ref.at[c, :, :, lanes] if c < 3 else rho_ref.at[:, :, lanes]
            copies.append(
                pltpu.make_async_copy(
                    src, state.at[2 * c + h, pl.ds(1, CX), pl.ds(0, CY), :], sems.at[2 * c + h]
                )
            )
    for copy in copies:
        copy.start()
    fetch = pltpu.make_async_copy(force_ref.at[:, pl.ds(0, PLANES)], grid_ref, sems.at[8])
    fetch.start()
    for j in range(8):
        fill = 0.0 if j < 6 else 1.0
        state[j, :, 32:40, :] = jnp.full((PLANES, 8, 128), fill, F32)
        state[j, 35, 0:32, :] = jnp.full((32, 128), fill, F32)
        state[j, 0] = left_ref[ROWS * j : ROWS * (j + 1), :]
        state[j, 33] = right_ref[2 * ROWS * j : 2 * ROWS * j + ROWS, :]
        state[j, 34] = right_ref[2 * ROWS * j + ROWS : 2 * ROWS * (j + 1), :]
        state[j, 1:33, 39, :] = below_ref[CX * j : CX * (j + 1), :]
        state[j, 1:33, 32, :] = above_ref[2 * CX * j : 2 * CX * j + CX, :]
        state[j, 1:33, 33, :] = above_ref[2 * CX * j + CX : 2 * CX * (j + 1), :]
    lo, ro = 8 * ROWS, 16 * ROWS
    ends = [
        scalar(left_ref[lo + 15 : lo + 16, :]) // 128, (scalar(left_ref[lo + 23 : lo + 24, :]) + 127) // 128,
        tiles_of(right_ref, ro),
    ] + [tiles_of(ref, base + LIST * i) for ref, base in ((left_ref, lo), (right_ref, ro)) for i in (1, 2)]
    fetch.wait()
    spread_edge(left_ref, lo, ends[0], ends[1], -1, 0, grid_ref)
    spread_edge(right_ref, ro, 0, ends[2], 1, 0, grid_ref)
    spread_edge(left_ref, lo + LIST, 0, ends[3], -1, -1, grid_ref)
    spread_edge(left_ref, lo + 2 * LIST, 0, ends[4], -1, 1, grid_ref)
    spread_edge(right_ref, ro + LIST, 0, ends[5], 1, -1, grid_ref)
    spread_edge(right_ref, ro + 2 * LIST, 0, ends[6], 1, 1, grid_ref)
    for copy in copies:
        copy.wait()

    def group(g, carry):
        e = 3 * g
        planes = pl.ds(e, 3)
        for h in range(2):
            half_over = 0.5 / state[6 + h, planes]
            for c in range(3):
                j = 2 * c + h
                value = state[j, planes] + grid_ref[j, planes] * half_over
                state[j, planes] = value
                flat = jnp.concatenate([value.reshape(3 * ROWS, 128), jnp.zeros((8, 128), F32)], axis=0)
                high, low = split(flat.T)
                rows = slice(128 * j, 128 * j + 128)
                ut_ref[rows, pl.ds(pl.multiple_of(128 * g, 128), 128)] = high
                ut_ref[rows, pl.ds(pl.multiple_of(128 * (GROUPS + REACH + g), 128), 128)] = low
        return carry

    lax.fori_loop(0, GROUPS, group, 0)
    outs = []
    for c in range(3):
        for h in range(2):
            outs.append(
                pltpu.make_async_copy(
                    state.at[2 * c + h, pl.ds(1, CX), pl.ds(0, CY), :],
                    out_ref.at[c, :, :, pl.ds(128 * h, 128)],
                    out_sem.at[2 * c + h],
                )
            )
    for copy in outs:
        copy.start()

    depth = 128 * (GROUPS + REACH)
    for part in range(2):
        start = depth * part + 128 * GROUPS
        ut_ref[:, start : start + 128 * REACH] = jnp.zeros((768, 128 * REACH), BF16)
    sorted_ref[...] = jnp.zeros(sorted_ref.shape, F32)

    def chunk(j, carry):
        lanes = pl.ds(pl.multiple_of(256 * j, 256), 256)
        (weight_x, weight_y, weight_z), _, (base_x, base_y, base_z) = decode(pair_of(list_ref, j))
        wy, wz = y_table(base_y, weight_y), z_table(base_z, weight_z)
        first_group = span_ref[2 * j] // 3
        high_x = span_ref[2 * j + 1]

        def window(w, sums):
            g = first_group + REACH * w
            wx_ref[...] = x_table(16, base_x, 3 * g, weight_x)
            for i in range(REACH):
                three = [wx_ref[e : e + 1, :] * wy for e in range(3 * i, 3 * i + 3)]
                high, low = split(jnp.concatenate(three + [jnp.zeros((8, 256), F32)], axis=0))
                a_ref[128 * i : 128 * i + 128, :] = high
                a_ref[128 * (REACH + i) : 128 * (REACH + i) + 128, :] = low
            wide = 128 * REACH
            ut_high = ut_ref[:, pl.ds(pl.multiple_of(128 * g, 128), wide)]
            ut_low = ut_ref[:, pl.ds(pl.multiple_of(depth + 128 * g, 128), wide)]
            high, low = a_ref[:wide, :], a_ref[wide:, :]
            picked = (
                jnp.dot(ut_high, high, preferred_element_type=F32)
                + jnp.dot(ut_high, low, preferred_element_type=F32)
                + jnp.dot(ut_low, high, preferred_element_type=F32)
            )
            return tuple(
                total + jnp.sum(picked[256 * c : 256 * c + 256] * wz, axis=0, keepdims=True)
                for c, total in enumerate(sums)
            )

        windows = (high_x + 4 - 3 * first_group + 3 * REACH - 1) // (3 * REACH)
        sums = lax.fori_loop(0, windows, window, tuple(jnp.zeros((1, 256), F32) for _ in range(3)))
        for c in range(3):
            sorted_ref[c : c + 1, lanes] = sums[c]
        return carry

    lax.fori_loop(0, (count + 1) // 2, chunk, 0)

    parts = jnp.concatenate([p.astype(F32) for p in split3(sorted_ref[...])], axis=0).astype(BF16)
    place = lax.broadcasted_iota(jnp.int32, (2048, 128), 0).astype(F32)
    vel_ref[...] = jnp.zeros(vel_ref.shape, F32)

    def back(t, carry):
        pick = jnp.concatenate(
            [jnp.where(place == pos_ref[pl.ds(2 * t + h, 1), :], 1.0, 0.0).astype(BF16) for h in range(2)], axis=1
        )
        sums = jnp.dot(parts, pick, preferred_element_type=F32)
        sums = sums[0:8] + sums[8:16] + sums[16:24]
        for h in range(2):
            for c in range(3):
                vel_ref[c, pl.ds(2 * t + h, 1), :] = sums[c : c + 1, 128 * h : 128 * h + 128]
        return carry

    lax.fori_loop(0, (count + 1) // 2, back, 0)
    for copy in outs:
        copy.wait()


def finish(count, span, markers, pos, u_old, density, below, above, left, right, grid):
    slots = pos.shape[0]
    return pl.pallas_call(
        finish_kernel,
        out_shape=[jax.ShapeDtypeStruct(u_old.shape, F32), jax.ShapeDtypeStruct((3, slots, 128), F32)],
        in_specs=[SMEM, SMEM, VMEM, VMEM] + [ANY, ANY] + [VMEM] * 4 + [ANY],
        out_specs=[ANY, VMEM],
        scratch_shapes=[
            pltpu.VMEM((6, PLANES, ROWS, 128), F32),
            pltpu.VMEM((8, PLANES, ROWS, 128), F32),
            pltpu.VMEM((768, 2 * 128 * (GROUPS + REACH)), BF16),
            pltpu.VMEM((2 * 128 * REACH, 256), BF16),
            pltpu.VMEM((16, 256), F32),
            pltpu.VMEM((8, 128 * slots), F32),
            pltpu.SemaphoreType.DMA((9,)),
            pltpu.SemaphoreType.DMA((6,)),
        ],
        cost_estimate=pl.CostEstimate(flops=6_000_000_000, bytes_accessed=12_000_000, transcendentals=0),
        name="finish",
    )(count, span, markers, pos, u_old, density, below, above, left, right, grid)


def shift(value, axis, steps):
    count = lax.axis_size(axis)
    return lax.ppermute(value, axis, [(i, (i + steps) % count) for i in range(count)])


def on_device(u_old, density, offsets, forces, base_x, base_y, base_z, tile_count):
    arrays = (offsets, forces, base_x, base_y, base_z)
    to_next, to_previous = pack_y(tile_count, arrays, u_old, density)
    below = shift(to_next, "gy", 1)
    above = shift(to_previous, "gy", -1)
    markers, pos, span = sort(tile_count, arrays)
    to_next, to_previous = pack_x(u_old, density, below, above, markers)
    left = shift(to_next, "gx", 1)
    right = shift(to_previous, "gx", -1)
    grid = spread(tile_count, span, markers, below, above)
    return finish(tile_count, span, markers, pos, u_old, density, below, above, left, right, grid)


def solution(mesh):
    in_specs = (
        P(None, "gx", "gy", None),
        P("gx", "gy", None),
        P(None, ("gx", "gy"), None),
        P(None, ("gx", "gy"), None),
        P(("gx", "gy"), None),
        P(("gx", "gy"), None),
        P(("gx", "gy"), None),
        P(("gx", "gy")),
    )
    out_specs = (P(None, "gx", "gy", None), P(None, ("gx", "gy"), None))
    return jax.shard_map(
        on_device, mesh=mesh, in_specs=in_specs, out_specs=out_specs, check_vma=False
    )
```

profile of v0, /device:TPU:24, one launch (start us, length us, event | category | flops | bytes accessed | tf_op | source)
XLA Modules:
  0.0 58.5 jit_solution(13632980060608941480)
XLA Ops:
  1.3 3.9 %pack_y.1 = (f32[384,128]{1,0:T(8,128)}, f32[640,128]{1,0:T(8,128)}) custom-call(s32[1]{0:T(128)S(6)} %copy.10.count_ref, f32[3,16,128]{2,1,0:T(8,128)} %off_ref.3, f32[3,16,128]{2,1,0:T(8,128)} %force_ref.3, s32[16,128]{1,0:T(8,128)} %bx_ref.3, s32[16,128]{1,0:T(8,128)} %by_ref.3, s32[16,128]{1,0:T(8,128)} %bz_ref.3, f32[3,32,32,256]{3,2,1,0:T(8,128)} %u_ref.5, ...), custom_call_target="tpu_custom_call" | custom-call | tf_op jit(solution)/shard_map/pack_y/pallas_call | solution.py:180
  5.1 6.9 %collective-permute-start.1 = (f32[640,128]{1,0:T(8,128)}, f32[640,128]{1,0:T(8,128)S(1)}, u32[]{:S(2)}, u32[]{:S(2)}) collective-permute-start(f32[640,128]{1,0:T(8,128)} %get-tuple-element.13), channel_id=1, source_target_pairs={{0,15},{1,0},{2,1},{3,2},{4,3},{5,4},{6,5},{7,6},{8,7},{9,8},{10,9... | collective-permute-start | bytes 983048 | tf_op jit(solution)/shard_map/ppermute | solution.py:545
  12.0 0.0 collective-permute-start
  12.0 4.3 %sort.1 = (f32[128,128]{1,0:T(8,128)}, f32[16,128]{1,0:T(8,128)}, s32[16]{0:T(128)}) custom-call(s32[1]{0:T(128)S(6)} %copy.10.count_ref, f32[3,16,128]{2,1,0:T(8,128)} %off_ref.3, f32[3,16,128]{2,1,0:T(8,128)} %force_ref.3, s32[16,128]{1,0:T(8,128)} %bx_ref.3, s32[16,128]{1,0:T(8,128)} %by_ref.3, s32[16,128]{1,0:T(8,128)} %bz_ref.3), custom_call_target="tpu_custom_call" | custom-call | flops 3000000000 | bytes 400000 | tf_op jit(solution)/shard_map/sort/pallas_call | solution.py:230
  16.4 4.3 %collective-permute-done.below_ref = f32[384,128]{1,0:T(8,128)S(1)} collective-permute-done((f32[384,128]{1,0:T(8,128)}, f32[384,128]{1,0:T(8,128)S(1)}, u32[]{:S(2)}, u32[]{:S(2)}) %collective-permute-start) | collective-permute-done | bytes 196640 | tf_op jit(solution)/shard_map/ppermute | solution.py:545
  20.7 0.0 copy-start.1
  20.7 0.0 collective-permute-done.1.above_ref
  20.7 0.0 copy-start
  20.7 0.7 %copy-done.1 = f32[384,128]{1,0:T(8,128)} copy-done((f32[384,128]{1,0:T(8,128)}, f32[384,128]{1,0:T(8,128)S(1)}, u32[]{:S(2)}) %copy-start.1) | copy-done | bytes 196632
  21.4 0.1 copy-done
  21.5 3.1 %pack_x.1 = (f32[704,128]{1,0:T(8,128)}, f32[1024,128]{1,0:T(8,128)}) custom-call(f32[3,32,32,256]{3,2,1,0:T(8,128)} %u_ref.5, f32[32,32,256]{2,1,0:T(8,128)} %rho_ref.5, f32[384,128]{1,0:T(8,128)} %copy-done.1, f32[640,128]{1,0:T(8,128)} %copy-done, f32[128,128]{1,0:T(8,128)} %get-tuple-element.10.list_ref), custom_call_target="tpu_custom_call" | custom-call | tf_op jit(solution)/shard_map/pack_x/pallas_call | solution.py:276
  24.6 0.1 collective-permute-start.2
  24.7 1.7 %collective-permute-start.3 = (f32[1024,128]{1,0:T(8,128)}, f32[1024,128]{1,0:T(8,128)S(1)}, u32[]{:S(2)}, u32[]{:S(2)}) collective-permute-start(f32[1024,128]{1,0:T(8,128)} %get-tuple-element.15), channel_id=1, source_target_pairs={{0,240},{16,0},{32,16},{48,32},{64,48},{80,64},{96,80},{112,96},{1... | collective-permute-start | bytes 1572872 | tf_op jit(solution)/shard_map/ppermute | solution.py:545
  26.4 12.4 %spread.1.force_ref = f32[6,45,40,128]{3,2,1,0:T(8,128)} custom-call(s32[1]{0:T(128)S(6)} %copy.10.count_ref, s32[16]{0:T(128)} %get-tuple-element.9.span_ref, f32[128,128]{1,0:T(8,128)} %get-tuple-element.10.list_ref, f32[384,128]{1,0:T(8,128)} %copy-done.1, f32[640,128]{1,0:T(8,128)} %copy-done), custom_call_target="tpu_custom_call" | custom-call | flops 6000000000 | bytes 6000000 | tf_op jit(solution)/shard_map/spread/pallas_call | solution.py:369
  38.9 0.0 collective-permute-done.2.left_ref
  38.9 0.0 copy-start.3
  38.9 0.0 collective-permute-done.3.right_ref
  38.9 0.0 copy-start.2
  38.9 0.7 %copy-done.3 = f32[704,128]{1,0:T(8,128)} copy-done((f32[704,128]{1,0:T(8,128)}, f32[704,128]{1,0:T(8,128)S(1)}, u32[]{:S(2)}) %copy-start.3) | copy-done | bytes 360472
  39.6 0.2 copy-done.2
  39.8 18.7 %finish.1 = (f32[3,32,32,256]{3,2,1,0:T(8,128)}, f32[3,16,128]{2,1,0:T(8,128)}) custom-call(s32[1]{0:T(128)S(6)} %copy.10.count_ref, s32[16]{0:T(128)} %get-tuple-element.9.span_ref, f32[128,128]{1,0:T(8,128)} %get-tuple-element.10.list_ref, f32[16,128]{1,0:T(8,128)} %get-tuple-element.11.pos_ref, f32[3,32,32,256]{3,2,1,0:T(8,128)} %u_ref.5, ...), custom_call_target="tpu_custom_call" | custom-call | flops 6000000000 | bytes 12000000 | tf_op jit(solution)/shard_map/finish/pallas_call | solution.py:523
Async XLA Ops:
  5.1 15.5 %collective-permute-start.1 = (f32[640,128]{1,0:T(8,128)}, f32[640,128]{1,0:T(8,128)S(1)}, u32[]{:S(2)}, u32[]{:S(2)}) collective-permute-start(f32[640,128]{1,0:T(8,128)} %get-tuple-element.13), channel_id=1, source_target_pairs={{0,15},{1,0},{2,1},{3,2},{4,3},{5,4},{6,5},{7,6},{8,7},{9,8},{10,9... | collective-permute-start | bytes 983048 | tf_op jit(solution)/shard_map/ppermute | solution.py:545
  12.0 8.7 %collective-permute-start = (f32[384,128]{1,0:T(8,128)}, f32[384,128]{1,0:T(8,128)S(1)}, u32[]{:S(2)}, u32[]{:S(2)}) collective-permute-start(f32[384,128]{1,0:T(8,128)} %get-tuple-element.12), channel_id=1, source_target_pairs={{0,1},{1,2},{2,3},{3,4},{4,5},{5,6},{6,7},{7,8},{8,9},{9,10},{10,1... | collective-permute-start | bytes 589832 | tf_op jit(solution)/shard_map/ppermute | solution.py:545
  20.7 0.7 %copy-start.1 = (f32[384,128]{1,0:T(8,128)}, f32[384,128]{1,0:T(8,128)S(1)}, u32[]{:S(2)}) copy-start(f32[384,128]{1,0:T(8,128)S(1)} %collective-permute-done.below_ref) | copy-start | bytes 589828
  20.7 0.8 %copy-start = (f32[640,128]{1,0:T(8,128)}, f32[640,128]{1,0:T(8,128)S(1)}, u32[]{:S(2)}) copy-start(f32[640,128]{1,0:T(8,128)S(1)} %collective-permute-done.1.above_ref) | copy-start | bytes 983044
  24.6 14.3 %collective-permute-start.2 = (f32[704,128]{1,0:T(8,128)}, f32[704,128]{1,0:T(8,128)S(1)}, u32[]{:S(2)}, u32[]{:S(2)}) collective-permute-start(f32[704,128]{1,0:T(8,128)} %get-tuple-element.14), channel_id=1, source_target_pairs={{0,16},{16,32},{32,48},{48,64},{64,80},{80,96},{96,112},{112,128},... | collective-permute-start | bytes 1081352 | tf_op jit(solution)/shard_map/ppermute | solution.py:545
  24.7 14.2 %collective-permute-start.3 = (f32[1024,128]{1,0:T(8,128)}, f32[1024,128]{1,0:T(8,128)S(1)}, u32[]{:S(2)}, u32[]{:S(2)}) collective-permute-start(f32[1024,128]{1,0:T(8,128)} %get-tuple-element.15), channel_id=1, source_target_pairs={{0,240},{16,0},{32,16},{48,32},{64,48},{80,64},{96,80},{112,96},{1... | collective-permute-start | bytes 1572872 | tf_op jit(solution)/shard_map/ppermute | solution.py:545
  38.9 0.8 %copy-start.3 = (f32[704,128]{1,0:T(8,128)}, f32[704,128]{1,0:T(8,128)S(1)}, u32[]{:S(2)}) copy-start(f32[704,128]{1,0:T(8,128)S(1)} %collective-permute-done.2.left_ref) | copy-start | bytes 1081348
  38.9 0.9 %copy-start.2 = (f32[1024,128]{1,0:T(8,128)}, f32[1024,128]{1,0:T(8,128)S(1)}, u32[]{:S(2)}) copy-start(f32[1024,128]{1,0:T(8,128)S(1)} %collective-permute-done.3.right_ref) | copy-start | bytes 1572868
where the time goes:
time: 58.9 us; the launch traced here: 58.5 us
  Pallas kernels  42.4 us (72%)
  starting transfers between devices  8.68 us (15%)
  waiting for transfers between devices  4.33 us (7%)
  local copies, waits for them, and re-layouts  1.74 us (3%)
  between operations  1.33 us (2%)
    pallas_call x1, Pallas kernels, finish(): pl.pallas_call(finish_kernel, out_shape=[jax.ShapeDtypeStruct(u_old.shape...  18.7 us
    pallas_call x1, Pallas kernels, spread(): pl.pallas_call(spread_kernel, out_shape=jax.ShapeDtypeStruct((6, PLANES +...  12.4 us
    ppermute x4, starting transfers between devices, shift(): lax.ppermute(value, axis, [(i, (i + steps) % count) for i in range(count)])  8.68 us
    pallas_call x1, Pallas kernels, sort(): pl.pallas_call(sort_kernel, out_shape=[jax.ShapeDtypeStruct((LIST, 128),...  4.34 us
    ppermute x4, waiting for transfers between devices, shift(): lax.ppermute(value, axis, [(i, (i + steps) % count) for i in range(count)])  4.33 us
    pallas_call x1, Pallas kernels, pack_y(): pl.pallas_call(pack_y_kernel, out_shape=[jax.ShapeDtypeStruct((8 * CX + L...  3.86 us
    pallas_call x1, Pallas kernels, pack_x(): pl.pallas_call(pack_x_kernel, out_shape=[jax.ShapeDtypeStruct((8 * ROWS +...  3.09 us
    unnamed x8, local copies, waits for them, and re-layouts  1.74 us
  transfers between devices with their start and end apart: 4, of which 1 were waited for; matrix products, arithmetic and copies ran while one was open for 0% of the time, Pallas kernels for 29%

commit v1 on v0

--- a/solution.py
+++ b/solution.py
@@ -9,13 +9,15 @@
 CX, CY, ROWS, PLANES = 32, 32, 40, 36
 GROUPS = 12
 WINDOW = 9
+TALL = 368
 REACH = 4
 TILES = 16
 LIST = 8 * TILES
 F32, BF16 = jnp.float32, jnp.bfloat16
 VMEM = pl.BlockSpec(memory_space=pltpu.VMEM)
 SMEM = pl.BlockSpec(memory_space=pltpu.SMEM)
-ANY = pl.BlockSpec(memory_space=pl.ANY)
+HBM = pl.BlockSpec(memory_space=pltpu.MemorySpace.HBM)
+MIB = 2**20
 
 
 def stencil(frac):
@@ -73,7 +75,7 @@
     return spread_four(256, [(base_z + c - 1) & 255 for c in range(4)], weights)
 
 
-def payload_of(pay_ref, off_ref, force_ref, bx_ref, by_ref, bz_ref):
+def fill_payload(pay_ref, off_ref, force_ref, bx_ref, by_ref, bz_ref):
     for t in range(TILES):
         lanes = slice(128 * t, 128 * t + 128)
         for c in range(3):
@@ -83,6 +85,9 @@
         pay_ref[7:8, lanes] = by_ref[t : t + 1, :].astype(F32)
         pay_ref[14:15, lanes] = bz_ref[t : t + 1, :].astype(F32)
         pay_ref[15:16, lanes] = jnp.ones((1, 128), F32)
+
+
+def payload_of(pay_ref):
     first, second, third = split3(pay_ref[0:8, :])
     row8 = lax.broadcasted_iota(jnp.int32, first.shape, 0)
     second = jnp.where(row8 < 6, second.astype(F32), pay_ref[8:16, :])
@@ -132,9 +137,17 @@
 
 
 def pack_y_kernel(
-    count_ref, off_ref, force_ref, bx_ref, by_ref, bz_ref, u_ref, rho_ref, yn_ref, yp_ref,
-    slab, pay_ref, col_ref, sems,
+    count_ref, off_hbm, force_hbm, bx_hbm, by_hbm, bz_hbm, u_ref, rho_ref, yn_ref, yp_ref, pay_ref,
+    off_ref, force_ref, bx_ref, by_ref, bz_ref, slab, col_ref, sems,
 ):
+    loads = [
+        pltpu.make_async_copy(src, dst, sems.at[2, n])
+        for n, (src, dst) in enumerate(
+            zip((by_hbm, bx_hbm, bz_hbm, off_hbm, force_hbm), (by_ref, bx_ref, bz_ref, off_ref, force_ref))
+        )
+    ]
+    for load in loads:
+        load.start()
     copies = []
     for c in range(4):
         for h in range(2):
@@ -146,6 +159,8 @@
     for copy in copies:
         copy.start()
     count = count_ref[0]
+    for load in loads:
+        load.wait()
     tile = lax.broadcasted_iota(jnp.int32, (TILES, 128), 0)
     y = jnp.where(tile < count, by_ref[...], CY // 2)
     low, high = (y < 3).astype(F32), (y > CY - 4).astype(F32)
@@ -156,7 +171,8 @@
     before = jnp.dot(earlier, counts[:, 128:].astype(BF16), preferred_element_type=F32)
     place = counts[:, :128] + before - 1.0
     columns_of(low * (place[:TILES] + 1.0) + high * (place[TILES:] + 4097.0) - 1.0, col_ref)
-    payload = payload_of(pay_ref, off_ref, force_ref, bx_ref, by_ref, bz_ref)
+    fill_payload(pay_ref, off_ref, force_ref, bx_ref, by_ref, bz_ref)
+    payload = payload_of(pay_ref)
     ends = before + counts[:, 128:]
     for n, (ref, base, start) in enumerate(((yp_ref, 16 * CX, 0), (yn_ref, 8 * CX, 4096))):
         end = ends[TILES * n + TILES - 1 : TILES * n + TILES]
@@ -182,25 +198,31 @@
         out_shape=[
             jax.ShapeDtypeStruct((8 * CX + LIST, 128), F32),
             jax.ShapeDtypeStruct((16 * CX + LIST, 128), F32),
-        ],
-        in_specs=[SMEM] + [VMEM] * 5 + [ANY, ANY],
-        out_specs=[VMEM] * 2,
+            jax.ShapeDtypeStruct((16, 128 * TILES), F32),
+        ],
+        in_specs=[SMEM] + [HBM] * 7,
+        out_specs=[VMEM] * 3,
         scratch_shapes=[
+            pltpu.VMEM((3, TILES, 128), F32),
+            pltpu.VMEM((3, TILES, 128), F32),
+            pltpu.VMEM((TILES, 128), jnp.int32),
+            pltpu.VMEM((TILES, 128), jnp.int32),
+            pltpu.VMEM((TILES, 128), jnp.int32),
             pltpu.VMEM((2, 8, CX, 8, 128), F32),
-            pltpu.VMEM((16, 128 * TILES), F32),
             pltpu.VMEM((128 * TILES, 128), F32),
-            pltpu.SemaphoreType.DMA((2, 8)),
+            pltpu.SemaphoreType.DMA((3, 8)),
         ],
         name="pack_y",
     )(count, *arrays, u_old, density)
 
 
-def sort_kernel(
-    count_ref, off_ref, force_ref, bx_ref, by_ref, bz_ref, list_ref, pos_ref, span_ref, pay_ref, col_ref
-):
+def sort_kernel(count_ref, pay_ref, list_ref, pos_ref, span_ref, col_ref):
     count = count_ref[0]
+    list_ref[...] = jnp.zeros(list_ref.shape, F32)
     key_row = lax.broadcasted_iota(jnp.int32, (CX, 128), 0)
-    keys = [jnp.where(t < count, bx_ref[t : t + 1, :], 2 * CX) for t in range(TILES)]
+    keys = [
+        jnp.where(t < count, pay_ref[6:7, 128 * t : 128 * t + 128].astype(jnp.int32), 2 * CX) for t in range(TILES)
+    ]
     same = [(key_row == k).astype(F32) for k in keys]
     less = [(k < key_row).astype(F32) for k in keys]
     counts = jnp.dot(jnp.concatenate(same, axis=0).astype(BF16), running(), preferred_element_type=F32)
@@ -211,22 +233,23 @@
         pos_ref[t : t + 1, :] = jnp.sum(same[t] * (part[:, :128] + before), axis=0, keepdims=True) - 1.0
         before = before + part[:, 128:]
     columns_of(pos_ref[...], col_ref)
-    payload = payload_of(pay_ref, off_ref, force_ref, bx_ref, by_ref, bz_ref)
-
-    def chunk(j, carry):
-        parts = gather(payload, col_ref, j, 0, list_ref, 0)
-        there = parts[15:16] > 0.5
-        span_ref[2 * j] = jnp.min(jnp.where(there, parts[6:7], 255.0)).astype(jnp.int32)
-        span_ref[2 * j + 1] = scalar(jnp.where(there, parts[6:7], 0.0))
+    payload = payload_of(pay_ref)
+
+    def chunks(p, carry):
+        for j in (2 * p, 2 * p + 1):
+            parts = gather(payload, col_ref, j, 0, list_ref, 0)
+            there = parts[15:16] > 0.5
+            span_ref[2 * j] = jnp.min(jnp.where(there, parts[6:7], CX - 1.0)).astype(jnp.int32)
+            span_ref[2 * j + 1] = scalar(jnp.where(there, parts[6:7], 0.0))
         return carry
 
-    lax.fori_loop(0, (count + 1) // 2, chunk, 0)
+    lax.fori_loop(0, (count + 3) // 4, chunks, 0)
     list_ref[7:8, :] = smaller[3:4]
     list_ref[15:16, :] = smaller[CX - 3 : CX - 2]
     list_ref[23:24, :] = jnp.full((1, 128), (128 * count).astype(F32))
 
 
-def sort(count, arrays):
+def sort(count, payload):
     return pl.pallas_call(
         sort_kernel,
         out_shape=[
@@ -234,12 +257,13 @@
             jax.ShapeDtypeStruct((TILES, 128), F32),
             jax.ShapeDtypeStruct((TILES,), jnp.int32),
         ],
-        in_specs=[SMEM] + [VMEM] * 5,
+        in_specs=[SMEM, VMEM],
         out_specs=[VMEM, VMEM, SMEM],
-        scratch_shapes=[pltpu.VMEM((16, 128 * TILES), F32), pltpu.VMEM((128 * TILES, 128), F32)],
+        compiler_params=pltpu.CompilerParams(vmem_limit_bytes=8 * MIB),
+        scratch_shapes=[pltpu.VMEM((128 * TILES, 128), F32)],
         cost_estimate=pl.CostEstimate(flops=3_000_000_000, bytes_accessed=400_000, transcendentals=0),
         name="sort",
-    )(count, *arrays)
+    )(count, payload)
 
 
 def pack_x_kernel(u_ref, rho_ref, below_ref, above_ref, list_ref, xn_ref, xp_ref, sems):
@@ -279,78 +303,94 @@
             jax.ShapeDtypeStruct((8 * ROWS + 3 * LIST, 128), F32),
             jax.ShapeDtypeStruct((16 * ROWS + 3 * LIST, 128), F32),
         ],
-        in_specs=[ANY, ANY] + [VMEM] * 3,
+        in_specs=[HBM, HBM] + [VMEM] * 3,
         out_specs=[VMEM] * 2,
+        compiler_params=pltpu.CompilerParams(vmem_limit_bytes=8 * MIB),
         scratch_shapes=[pltpu.SemaphoreType.DMA((3, 8))],
         name="pack_x",
     )(u_old, density, below, above, markers)
 
 
-def spread_list(list_ref, chunks, span_ref, grid_ref, a_ref, b_ref, wx_ref):
-    def chunk(j, carry):
+def spread_list(list_ref, pairs, span_ref, grid_ref, a_ref, b_ref, wx_ref):
+    def tables(j, k):
         (weight_x, weight_y, weight_z), forces, (base_x, base_y, base_z) = decode(pair_of(list_ref, j))
         wy, wz = y_table(base_y, weight_y), z_table(base_z, weight_z)
         for c in range(3):
             high, low = split(wz * forces[c])
-            for part, value in enumerate((high, high, low)):
-                b_ref[256 * c : 256 * c + 256, 256 * part : 256 * part + 256] = value
-        low_x, high_x = span_ref[2 * j], span_ref[2 * j + 1]
-
-        def window(w, carry):
-            first = low_x + WINDOW * w
-            wx_ref[...] = x_table(16, base_x, first, weight_x)
-            flat = jnp.concatenate([wx_ref[e : e + 1, :] * wy for e in range(WINDOW)], axis=0)
-            high, low = split(flat)
-            for part, value in enumerate((high, low, high)):
-                a_ref[:, 256 * part : 256 * part + 256] = value
-            sums = lax.dot_general(
-                a_ref[...], b_ref[...], (((1,), (1,)), ((), ())), preferred_element_type=F32
+            b_ref[k, 0, 256 * c : 256 * c + 256, :] = high
+            b_ref[k, 1, 256 * c : 256 * c + 256, :] = low
+        return weight_x, base_x, wy
+
+    def window(first, weight_x, base_x, wy, k):
+        wx_ref[k] = x_table(16, base_x, first, weight_x)
+        rows = [wx_ref[k, e : e + 1, :] * wy for e in range(WINDOW)]
+        high, low = split(jnp.concatenate(rows + [jnp.zeros((TALL - WINDOW * ROWS, 256), F32)], axis=0))
+        a_ref[k, :TALL, :] = high
+        a_ref[k, TALL:, :] = low
+        across = (((1,), (1,)), ((), ()))
+        both = lax.dot_general(a_ref[k], b_ref[k, 0], across, preferred_element_type=F32)
+        rest = lax.dot_general(a_ref[k, :TALL, :], b_ref[k, 1], across, preferred_element_type=F32)
+        sums = (both[:TALL] + rest + both[TALL:])[: WINDOW * ROWS]
+        for j in range(6):
+            grid_ref[j, pl.ds(first, WINDOW)] += sums[:, 128 * j : 128 * j + 128].reshape(
+                WINDOW, ROWS, 128
             )
-            for j in range(6):
-                grid_ref[j, pl.ds(first, WINDOW)] += sums[:, 128 * j : 128 * j + 128].reshape(
-                    WINDOW, ROWS, 128
-                )
-            return carry
-
-        lax.fori_loop(0, (high_x + 4 - low_x + WINDOW - 1) // WINDOW, window, 0)
+
+    def two(p, carry):
+        both = [(tables(2 * p + k, k), k) for k in range(2)]
+        for table, k in both:
+            window(span_ref[2 * (2 * p + k)], *table, k)
+        for table, k in both:
+            low_x, high_x = span_ref[2 * (2 * p + k)], span_ref[2 * (2 * p + k) + 1]
+
+            def more(w, carry, table=table, k=k, low_x=low_x):
+                window(low_x + WINDOW * w, *table, k)
+                return carry
+
+            lax.fori_loop(1, (high_x + 4 - low_x + WINDOW - 1) // WINDOW, more, 0)
         return carry
 
-    lax.fori_loop(0, chunks, chunk, 0)
-
-
-def spread_edge(ref, base, first, last, dx, dy, grid_ref):
-    def tile(t, carry):
-        rows = pl.ds(pl.multiple_of(base + 8 * t, 8), 8)
-        (weight_x, weight_y, weight_z), forces, (base_x, base_y, base_z) = decode(ref[rows, :])
-        base_x, base_y = base_x + CX * dx, base_y + CY * dy
-        wz = z_table(base_z, weight_z)
+    lax.fori_loop(0, pairs, two, 0)
+
+
+def spread_edges(edges, grid_ref):
+    for edge in edges:
+        edge_tile(*edge[:3], *edge[4:], grid_ref)
+    for edge in edges:
+        lax.fori_loop(
+            edge[2] + 1, edge[3], lambda t, carry, e=edge: edge_tile(*e[:2], t, *e[4:], grid_ref) or carry, 0
+        )
+
+
+def edge_tile(ref, base, t, dx, dy, grid_ref):
+    rows = pl.ds(pl.multiple_of(base + 8 * t, 8), 8)
+    (weight_x, weight_y, weight_z), forces, (base_x, base_y, base_z) = decode(ref[rows, :])
+    base_x, base_y = base_x + CX * dx, base_y + CY * dy
+    wz = z_table(base_z, weight_z)
+    if dx == 0:
+        table = x_table(ROWS, base_x, 0, weight_x)
+        cells = (-1, 0, 1) if dy < 0 else (CY - 1, CY, CY + 1)
+        lines = [one_row(base_y, cell, weight_y) for cell in cells]
+    else:
+        table = y_table(base_y, weight_y)
+        cells = (-1, 0, 1) if dx < 0 else (CX - 1, CX, CX + 1)
+        lines = [one_row(base_x, cell, weight_x) for cell in cells]
+    a_high, a_low = split(jnp.concatenate([table * line for line in lines], axis=0))
+    b_high, b_low = split(jnp.concatenate([wz * force for force in forces], axis=0))
+    sums = lax.dot_general(
+        jnp.concatenate([a_high, a_low, a_high], axis=1),
+        jnp.concatenate([b_high, b_high, b_low], axis=1),
+        (((1,), (1,)), ((), ())),
+        preferred_element_type=F32,
+    )
+    for j in range(6):
+        part = sums[:, 128 * j : 128 * j + 128]
         if dx == 0:
-            table = x_table(ROWS, base_x, 0, weight_x)
-            cells = (-1, 0, 1) if dy < 0 else (CY - 1, CY, CY + 1)
-            lines = [one_row(base_y, cell, weight_y) for cell in cells]
+            for i, cell in enumerate(cells):
+                row = cell % ROWS
+                grid_ref[j, 0:PLANES, row, :] += part[ROWS * i : ROWS * i + PLANES]
         else:
-            table = y_table(base_y, weight_y)
-            cells = (-1, 0, 1) if dx < 0 else (CX - 1, CX, CX + 1)
-            lines = [one_row(base_x, cell, weight_x) for cell in cells]
-        a_high, a_low = split(jnp.concatenate([table * line for line in lines], axis=0))
-        b_high, b_low = split(jnp.concatenate([wz * force for force in forces], axis=0))
-        sums = lax.dot_general(
-            jnp.concatenate([a_high, a_low, a_high], axis=1),
-            jnp.concatenate([b_high, b_high, b_low], axis=1),
-            (((1,), (1,)), ((), ())),
-            preferred_element_type=F32,
-        )
-        for j in range(6):
-            part = sums[:, 128 * j : 128 * j + 128]
-            if dx == 0:
-                for i, cell in enumerate(cells):
-                    row = cell % ROWS
-                    grid_ref[j, 0:PLANES, row, :] += part[ROWS * i : ROWS * i + PLANES]
-            else:
-                grid_ref[j, cells[0] + 1 : cells[0] + 4] += part.reshape(3, ROWS, 128)
-        return carry
-
-    lax.fori_loop(first, last, tile, 0)
+            grid_ref[j, cells[0] + 1 : cells[0] + 4] += part.reshape(3, ROWS, 128)
 
 
 def tiles_of(ref, base):
@@ -360,9 +400,14 @@
 def spread_kernel(count_ref, span_ref, list_ref, below_ref, above_ref, grid_ref, a_ref, b_ref, wx_ref):
     for j in range(6):
         grid_ref[j] = jnp.zeros(grid_ref.shape[1:], F32)
-    spread_list(list_ref, (count_ref[0] + 1) // 2, span_ref, grid_ref, a_ref, b_ref, wx_ref)
-    spread_edge(below_ref, 8 * CX, 0, tiles_of(below_ref, 8 * CX), 0, -1, grid_ref)
-    spread_edge(above_ref, 16 * CX, 0, tiles_of(above_ref, 16 * CX), 0, 1, grid_ref)
+    spread_list(list_ref, (count_ref[0] + 3) // 4, span_ref, grid_ref, a_ref, b_ref, wx_ref)
+    spread_edges(
+        [
+            (below_ref, 8 * CX, 0, tiles_of(below_ref, 8 * CX), 0, -1),
+            (above_ref, 16 * CX, 0, tiles_of(above_ref, 16 * CX), 0, 1),
+        ],
+        grid_ref,
+    )
 
 
 def spread(count, span, markers, below, above):
@@ -371,10 +416,11 @@
         out_shape=jax.ShapeDtypeStruct((6, PLANES + WINDOW, ROWS, 128), F32),
         in_specs=[SMEM, SMEM] + [VMEM] * 3,
         out_specs=VMEM,
+        compiler_params=pltpu.CompilerParams(vmem_limit_bytes=16 * MIB),
         scratch_shapes=[
-            pltpu.VMEM((WINDOW * ROWS, 768), BF16),
-            pltpu.VMEM((768, 768), BF16),
-            pltpu.VMEM((16, 256), F32),
+            pltpu.VMEM((2, 2 * TALL, 256), BF16),
+            pltpu.VMEM((2, 2, 768, 256), BF16),
+            pltpu.VMEM((2, 16, 256), F32),
         ],
         cost_estimate=pl.CostEstimate(flops=6_000_000_000, bytes_accessed=6_000_000, transcendentals=0),
         name="spread",
@@ -398,8 +444,6 @@
             )
     for copy in copies:
         copy.start()
-    fetch = pltpu.make_async_copy(force_ref.at[:, pl.ds(0, PLANES)], grid_ref, sems.at[8])
-    fetch.start()
     for j in range(8):
         fill = 0.0 if j < 6 else 1.0
         state[j, :, 32:40, :] = jnp.full((PLANES, 8, 128), fill, F32)
@@ -415,13 +459,17 @@
         scalar(left_ref[lo + 15 : lo + 16, :]) // 128, (scalar(left_ref[lo + 23 : lo + 24, :]) + 127) // 128,
         tiles_of(right_ref, ro),
     ] + [tiles_of(ref, base + LIST * i) for ref, base in ((left_ref, lo), (right_ref, ro)) for i in (1, 2)]
-    fetch.wait()
-    spread_edge(left_ref, lo, ends[0], ends[1], -1, 0, grid_ref)
-    spread_edge(right_ref, ro, 0, ends[2], 1, 0, grid_ref)
-    spread_edge(left_ref, lo + LIST, 0, ends[3], -1, -1, grid_ref)
-    spread_edge(left_ref, lo + 2 * LIST, 0, ends[4], -1, 1, grid_ref)
-    spread_edge(right_ref, ro + LIST, 0, ends[5], 1, -1, grid_ref)
-    spread_edge(right_ref, ro + 2 * LIST, 0, ends[6], 1, 1, grid_ref)
+    spread_edges(
+        [
+            (left_ref, lo, jnp.minimum(ends[0], TILES - 1), ends[1], -1, 0),
+            (right_ref, ro, 0, ends[2], 1, 0),
+            (left_ref, lo + LIST, 0, ends[3], -1, -1),
+            (left_ref, lo + 2 * LIST, 0, ends[4], -1, 1),
+            (right_ref, ro + LIST, 0, ends[5], 1, -1),
+            (right_ref, ro + 2 * LIST, 0, ends[6], 1, 1),
+        ],
+        grid_ref,
+    )
     for copy in copies:
         copy.wait()
 
@@ -461,59 +509,68 @@
         ut_ref[:, start : start + 128 * REACH] = jnp.zeros((768, 128 * REACH), BF16)
     sorted_ref[...] = jnp.zeros(sorted_ref.shape, F32)
 
-    def chunk(j, carry):
-        lanes = pl.ds(pl.multiple_of(256 * j, 256), 256)
+    wide = 128 * REACH
+
+    def tables(j):
         (weight_x, weight_y, weight_z), _, (base_x, base_y, base_z) = decode(pair_of(list_ref, j))
-        wy, wz = y_table(base_y, weight_y), z_table(base_z, weight_z)
-        first_group = span_ref[2 * j] // 3
-        high_x = span_ref[2 * j + 1]
-
-        def window(w, sums):
-            g = first_group + REACH * w
-            wx_ref[...] = x_table(16, base_x, 3 * g, weight_x)
-            for i in range(REACH):
-                three = [wx_ref[e : e + 1, :] * wy for e in range(3 * i, 3 * i + 3)]
-                high, low = split(jnp.concatenate(three + [jnp.zeros((8, 256), F32)], axis=0))
-                a_ref[128 * i : 128 * i + 128, :] = high
-                a_ref[128 * (REACH + i) : 128 * (REACH + i) + 128, :] = low
-            wide = 128 * REACH
-            ut_high = ut_ref[:, pl.ds(pl.multiple_of(128 * g, 128), wide)]
-            ut_low = ut_ref[:, pl.ds(pl.multiple_of(depth + 128 * g, 128), wide)]
-            high, low = a_ref[:wide, :], a_ref[wide:, :]
-            picked = (
-                jnp.dot(ut_high, high, preferred_element_type=F32)
-                + jnp.dot(ut_high, low, preferred_element_type=F32)
-                + jnp.dot(ut_low, high, preferred_element_type=F32)
-            )
-            return tuple(
-                total + jnp.sum(picked[256 * c : 256 * c + 256] * wz, axis=0, keepdims=True)
-                for c, total in enumerate(sums)
-            )
-
-        windows = (high_x + 4 - 3 * first_group + 3 * REACH - 1) // (3 * REACH)
-        sums = lax.fori_loop(0, windows, window, tuple(jnp.zeros((1, 256), F32) for _ in range(3)))
-        for c in range(3):
-            sorted_ref[c : c + 1, lanes] = sums[c]
+        return weight_x, base_x, y_table(base_y, weight_y), z_table(base_z, weight_z)
+
+    def window(g, weight_x, base_x, wy, wz, k):
+        wx_ref[k] = x_table(16, base_x, 3 * g, weight_x)
+        for i in range(REACH):
+            three = [wx_ref[k, e : e + 1, :] * wy for e in range(3 * i, 3 * i + 3)]
+            high, low = split(jnp.concatenate(three + [jnp.zeros((8, 256), F32)], axis=0))
+            a_ref[k, 128 * i : 128 * i + 128, :] = high
+            a_ref[k, 128 * (REACH + i) : 128 * (REACH + i) + 128, :] = low
+        ut_high = ut_ref[:, pl.ds(pl.multiple_of(128 * g, 128), wide)]
+        ut_low = ut_ref[:, pl.ds(pl.multiple_of(depth + 128 * g, 128), wide)]
+        high, low = a_ref[k, :wide, :], a_ref[k, wide:, :]
+        picked = (
+            jnp.dot(ut_high, high, preferred_element_type=F32)
+            + jnp.dot(ut_high, low, preferred_element_type=F32)
+            + jnp.dot(ut_low, high, preferred_element_type=F32)
+        )
+        return [jnp.sum(picked[256 * c : 256 * c + 256] * wz, axis=0, keepdims=True) for c in range(3)]
+
+    def two(p, carry):
+        both = [(tables(2 * p + k), k) for k in range(2)]
+        for table, k in both:
+            j = 2 * p + k
+            lanes = pl.ds(pl.multiple_of(256 * j, 256), 256)
+            for c, value in enumerate(window(span_ref[2 * j] // 3, *table, k)):
+                sorted_ref[c : c + 1, lanes] = value
+        for table, k in both:
+            j = 2 * p + k
+            lanes = pl.ds(pl.multiple_of(256 * j, 256), 256)
+            first, high_x = span_ref[2 * j] // 3, span_ref[2 * j + 1]
+
+            def more(w, carry, table=table, k=k, lanes=lanes, first=first):
+                for c, value in enumerate(window(first + REACH * w, *table, k)):
+                    sorted_ref[c : c + 1, lanes] += value
+                return carry
+
+            lax.fori_loop(1, (high_x + 4 - 3 * first + 3 * REACH - 1) // (3 * REACH), more, 0)
         return carry
 
-    lax.fori_loop(0, (count + 1) // 2, chunk, 0)
+    lax.fori_loop(0, (count + 3) // 4, two, 0)
 
     parts = jnp.concatenate([p.astype(F32) for p in split3(sorted_ref[...])], axis=0).astype(BF16)
     place = lax.broadcasted_iota(jnp.int32, (2048, 128), 0).astype(F32)
     vel_ref[...] = jnp.zeros(vel_ref.shape, F32)
 
-    def back(t, carry):
-        pick = jnp.concatenate(
-            [jnp.where(place == pos_ref[pl.ds(2 * t + h, 1), :], 1.0, 0.0).astype(BF16) for h in range(2)], axis=1
-        )
-        sums = jnp.dot(parts, pick, preferred_element_type=F32)
-        sums = sums[0:8] + sums[8:16] + sums[16:24]
-        for h in range(2):
-            for c in range(3):
-                vel_ref[c, pl.ds(2 * t + h, 1), :] = sums[c : c + 1, 128 * h : 128 * h + 128]
+    def back(p, carry):
+        for t in (4 * p, 4 * p + 2):
+            pick = jnp.concatenate(
+                [jnp.where(place == pos_ref[pl.ds(t + h, 1), :], 1.0, 0.0).astype(BF16) for h in range(2)], axis=1
+            )
+            sums = jnp.dot(parts, pick, preferred_element_type=F32)
+            sums = sums[0:8] + sums[8:16] + sums[16:24]
+            for h in range(2):
+                for c in range(3):
+                    vel_ref[c, pl.ds(t + h, 1), :] = sums[c : c + 1, 128 * h : 128 * h + 128]
         return carry
 
-    lax.fori_loop(0, (count + 1) // 2, back, 0)
+    lax.fori_loop(0, (count + 3) // 4, back, 0)
     for copy in outs:
         copy.wait()
 
@@ -522,22 +579,27 @@
     slots = pos.shape[0]
     return pl.pallas_call(
         finish_kernel,
-        out_shape=[jax.ShapeDtypeStruct(u_old.shape, F32), jax.ShapeDtypeStruct((3, slots, 128), F32)],
-        in_specs=[SMEM, SMEM, VMEM, VMEM] + [ANY, ANY] + [VMEM] * 4 + [ANY],
-        out_specs=[ANY, VMEM],
+        out_shape=[
+            jax.ShapeDtypeStruct(u_old.shape, F32),
+            jax.ShapeDtypeStruct((3, slots, 128), F32),
+            jax.ShapeDtypeStruct(grid.shape, F32),
+        ],
+        input_output_aliases={10: 2},
+        in_specs=[SMEM, SMEM, VMEM, VMEM] + [HBM, HBM] + [VMEM] * 5,
+        out_specs=[HBM, VMEM, VMEM],
+        compiler_params=pltpu.CompilerParams(vmem_limit_bytes=36 * MIB),
         scratch_shapes=[
-            pltpu.VMEM((6, PLANES, ROWS, 128), F32),
             pltpu.VMEM((8, PLANES, ROWS, 128), F32),
             pltpu.VMEM((768, 2 * 128 * (GROUPS + REACH)), BF16),
-            pltpu.VMEM((2 * 128 * REACH, 256), BF16),
-            pltpu.VMEM((16, 256), F32),
+            pltpu.VMEM((2, 2 * 128 * REACH, 256), BF16),
+            pltpu.VMEM((2, 16, 256), F32),
             pltpu.VMEM((8, 128 * slots), F32),
             pltpu.SemaphoreType.DMA((9,)),
             pltpu.SemaphoreType.DMA((6,)),
         ],
         cost_estimate=pl.CostEstimate(flops=6_000_000_000, bytes_accessed=12_000_000, transcendentals=0),
         name="finish",
-    )(count, span, markers, pos, u_old, density, below, above, left, right, grid)
+    )(count, span, markers, pos, u_old, density, below, above, left, right, grid)[:2]
 
 
 def shift(value, axis, steps):
@@ -547,15 +609,15 @@
 
 def on_device(u_old, density, offsets, forces, base_x, base_y, base_z, tile_count):
     arrays = (offsets, forces, base_x, base_y, base_z)
-    to_next, to_previous = pack_y(tile_count, arrays, u_old, density)
+    to_next, to_previous, payload = pack_y(tile_count, arrays, u_old, density)
     below = shift(to_next, "gy", 1)
     above = shift(to_previous, "gy", -1)
-    markers, pos, span = sort(tile_count, arrays)
+    markers, pos, span = sort(tile_count, payload)
     to_next, to_previous = pack_x(u_old, density, below, above, markers)
     left = shift(to_next, "gx", 1)
     right = shift(to_previous, "gx", -1)
     grid = spread(tile_count, span, markers, below, above)
-    return finish(tile_count, span, markers, pos, u_old, density, below, above, left, right, grid)
+    return finish(tile_count, span, markers, pos, u_old, density, below, above, left, right, grid)[:2]
 
 
 def solution(mesh):

time: 58.9 us -> 47.5 us (0.81)
  the two profiles are of different devices: /device:TPU:24 before, /device:TPU:25 now
where the time goes in v1:
time: 47.5 us; the launch traced here: 47.4 us
  Pallas kernels  22.9 us (48%)
  waiting for transfers between devices  11.7 us (25%)
  starting transfers between devices  10.5 us (22%)
  between operations  1.49 us (3%)
  local copies, waits for them, and re-layouts  0.91 us (2%)
    ppermute x4, waiting for transfers between devices, shift(): lax.ppermute(value, axis, [(i, (i + steps) % count) for i in range(count)])  11.7 us
    pallas_call x1, Pallas kernels, finish(): pl.pallas_call(finish_kernel, out_shape=[jax.ShapeDtypeStruct(u_old.shape...  11.4 us
    ppermute x4, starting transfers between devices, shift(): lax.ppermute(value, axis, [(i, (i + steps) % count) for i in range(count)])  10.5 us
    pallas_call x1, Pallas kernels, spread(): pl.pallas_call(spread_kernel, out_shape=jax.ShapeDtypeStruct((6, PLANES +...  5.45 us
    pallas_call x1, Pallas kernels, pack_y(): pl.pallas_call(pack_y_kernel, out_shape=[jax.ShapeDtypeStruct((8 * CX + L...  3.62 us
    pallas_call x1, Pallas kernels, sort(): pl.pallas_call(sort_kernel, out_shape=[jax.ShapeDtypeStruct((LIST, 128),...  2 us
  transfers between devices with their start and end apart: 4, of which 2 were waited for; matrix products, arithmetic and copies ran while one was open for 0% of the time, Pallas kernels for 16%

profile of v1, /device:TPU:25, one launch (start us, length us, event | category | flops | bytes accessed | tf_op | source)
XLA Modules:
  0.0 47.4 jit_solution(3036129565410992455)
XLA Ops:
  1.3 3.6 %pack_y.1 = (f32[384,128]{1,0:T(8,128)}, f32[640,128]{1,0:T(8,128)}, f32[16,2048]{1,0:T(8,128)}) custom-call(s32[1]{0:T(128)S(6)} %copy.12.count_ref, f32[3,16,128]{2,1,0:T(8,128)} %off_hbm.1, f32[3,16,128]{2,1,0:T(8,128)} %force_hbm.1, s32[16,128]{1,0:T(8,128)} %bx_hbm.1, s32[16,128]{1,0:T(8,128)} %by_hbm.1, s32[16,128]{1,0:T(8,128)} %bz_hbm.1, ...), custom_call_target="tpu_custom_call" | custom-call | tf_op jit(solution)/shard_map/pack_y/pallas_call | solution.py:196
  4.9 6.6 %collective-permute-start.1 = (f32[640,128]{1,0:T(8,128)}, f32[640,128]{1,0:T(8,128)S(1)}, u32[]{:S(2)}, u32[]{:S(2)}) collective-permute-start(f32[640,128]{1,0:T(8,128)} %get-tuple-element.17), channel_id=1, source_target_pairs={{0,15},{1,0},{2,1},{3,2},{4,3},{5,4},{6,5},{7,6},{8,7},{9,8},{10,9... | collective-permute-start | bytes 983048 | tf_op jit(solution)/shard_map/ppermute | solution.py:607
  11.5 0.0 collective-permute-start
  11.5 0.0 copy-start.2
  11.5 0.9 %copy-done.2 = f32[16,2048]{1,0:T(8,128)S(1)} copy-done((f32[16,2048]{1,0:T(8,128)S(1)}, f32[16,2048]{1,0:T(8,128)}, u32[]{:S(2)}) %copy-start.2) | copy-done | bytes 131096
  12.4 0.0 copy-start
  12.4 0.0 copy-start.1
  12.4 2.0 %sort.1 = (f32[128,128]{1,0:T(8,128)S(1)}, f32[16,128]{1,0:T(8,128)S(1)}, s32[16]{0:T(128)S(1)}) custom-call(s32[1]{0:T(128)S(6)} %copy.12.count_ref, f32[16,2048]{1,0:T(8,128)S(1)} %copy-done.2), custom_call_target="tpu_custom_call" | custom-call | flops 3000000000 | bytes 400000 | tf_op jit(solution)/shard_map/sort/pallas_call | solution.py:253
  14.4 4.9 %collective-permute-done.below_ref = f32[384,128]{1,0:T(8,128)S(1)} collective-permute-done((f32[384,128]{1,0:T(8,128)}, f32[384,128]{1,0:T(8,128)S(1)}, u32[]{:S(2)}, u32[]{:S(2)}) %collective-permute-start) | collective-permute-done | bytes 196640 | tf_op jit(solution)/shard_map/ppermute | solution.py:607
  19.3 0.0 collective-permute-done.1.above_ref
  19.3 0.0 copy-done
  19.3 0.0 copy-done.1
  19.3 0.4 pack_x.1
  19.8 3.9 %collective-permute-start.2 = (f32[704,128]{1,0:T(8,128)S(1)}, f32[704,128]{1,0:T(8,128)S(1)}, u32[]{:S(2)}, u32[]{:S(2)}) collective-permute-start(f32[704,128]{1,0:T(8,128)S(1)} %get-tuple-element.18), channel_id=1, source_target_pairs={{0,16},{16,32},{32,48},{48,64},{64,80},{80,96},{96,112},{112,128},... | collective-permute-start | bytes 1081352 | tf_op jit(solution)/shard_map/ppermute | solution.py:607
  23.7 0.0 collective-permute-start.3
  23.7 5.4 %spread.1.force_ref = f32[6,45,40,128]{3,2,1,0:T(8,128)S(1)} custom-call(s32[1]{0:T(128)S(6)} %copy.12.count_ref, s32[16]{0:T(128)S(1)} %get-tuple-element.13.span_ref, f32[128,128]{1,0:T(8,128)S(1)} %get-tuple-element.14.list_ref, f32[384,128]{1,0:T(8,128)S(1)} %collective-permute-done.below_ref, f32[640,128]{1,0:T(8,128)S(1)} %collective-permute-done.1.above_ref), custom_call_target="tpu_custom_call" | custom-call | flops 6000000000 | bytes 6000000 | tf_op jit(solution)/shard_map/spread/pallas_call | solution.py:414
  29.1 0.0 collective-permute-done.2.left_ref
  29.1 6.7 %collective-permute-done.3.right_ref = f32[1024,128]{1,0:T(8,128)S(1)} collective-permute-done((f32[1024,128]{1,0:T(8,128)S(1)}, f32[1024,128]{1,0:T(8,128)S(1)}, u32[]{:S(2)}, u32[]{:S(2)}) %collective-permute-start.3) | collective-permute-done | bytes 524320 | tf_op jit(solution)/shard_map/ppermute | solution.py:607
  35.9 11.4 %finish.1 = (f32[3,32,32,256]{3,2,1,0:T(8,128)}, f32[3,16,128]{2,1,0:T(8,128)}, f32[6,45,40,128]{3,2,1,0:T(8,128)S(1)}) custom-call(s32[1]{0:T(128)S(6)} %copy.12.count_ref, s32[16]{0:T(128)S(1)} %get-tuple-element.13.span_ref, f32[128,128]{1,0:T(8,128)S(1)} %get-tuple-element.14.list_ref, ...), custom_call_target="tpu_custom_call", output_to_operand_aliasing={{2}: (10, {})} | custom-call | flops 6000000000 | bytes 12000000 | tf_op jit(solution)/shard_map/finish/pallas_call | solution.py:580
Async XLA Ops:
  4.9 14.4 %collective-permute-start.1 = (f32[640,128]{1,0:T(8,128)}, f32[640,128]{1,0:T(8,128)S(1)}, u32[]{:S(2)}, u32[]{:S(2)}) collective-permute-start(f32[640,128]{1,0:T(8,128)} %get-tuple-element.17), channel_id=1, source_target_pairs={{0,15},{1,0},{2,1},{3,2},{4,3},{5,4},{6,5},{7,6},{8,7},{9,8},{10,9... | collective-permute-start | bytes 983048 | tf_op jit(solution)/shard_map/ppermute | solution.py:607
  11.5 7.8 %collective-permute-start = (f32[384,128]{1,0:T(8,128)}, f32[384,128]{1,0:T(8,128)S(1)}, u32[]{:S(2)}, u32[]{:S(2)}) collective-permute-start(f32[384,128]{1,0:T(8,128)} %get-tuple-element.16), channel_id=1, source_target_pairs={{0,1},{1,2},{2,3},{3,4},{4,5},{5,6},{6,7},{7,8},{8,9},{9,10},{10,1... | collective-permute-start | bytes 589832 | tf_op jit(solution)/shard_map/ppermute | solution.py:607
  11.5 0.9 %copy-start.2 = (f32[16,2048]{1,0:T(8,128)S(1)}, f32[16,2048]{1,0:T(8,128)}, u32[]{:S(2)}) copy-start(f32[16,2048]{1,0:T(8,128)} %get-tuple-element.12.pay_ref) | copy-start | bytes 393220
  12.4 6.9 %copy-start = (f32[3,32,32,256]{3,2,1,0:T(8,128)S(1)}, f32[3,32,32,256]{3,2,1,0:T(8,128)}, u32[]{:S(2)}) copy-start(f32[3,32,32,256]{3,2,1,0:T(8,128)} %u_ref.5) | copy-start | bytes 9437188
  12.4 6.9 %copy-start.1 = (f32[32,32,256]{2,1,0:T(8,128)S(1)}, f32[32,32,256]{2,1,0:T(8,128)}, u32[]{:S(2)}) copy-start(f32[32,32,256]{2,1,0:T(8,128)} %rho_ref.5) | copy-start | bytes 3145732
  19.8 9.3 %collective-permute-start.2 = (f32[704,128]{1,0:T(8,128)S(1)}, f32[704,128]{1,0:T(8,128)S(1)}, u32[]{:S(2)}, u32[]{:S(2)}) collective-permute-start(f32[704,128]{1,0:T(8,128)S(1)} %get-tuple-element.18), channel_id=1, source_target_pairs={{0,16},{16,32},{32,48},{48,64},{64,80},{80,96},{96,112},{112,128},... | collective-permute-start | bytes 1081352 | tf_op jit(solution)/shard_map/ppermute | solution.py:607
  23.7 12.2 %collective-permute-start.3 = (f32[1024,128]{1,0:T(8,128)S(1)}, f32[1024,128]{1,0:T(8,128)S(1)}, u32[]{:S(2)}, u32[]{:S(2)}) collective-permute-start(f32[1024,128]{1,0:T(8,128)S(1)} %get-tuple-element.19), channel_id=1, source_target_pairs={{0,240},{16,0},{32,16},{48,32},{64,48},{80,64},{96,80},{112,96},{1... | collective-permute-start | bytes 1572872 | tf_op jit(solution)/shard_map/ppermute | solution.py:607

commit v2 on v1

--- a/solution.py
+++ b/solution.py
@@ -397,24 +397,17 @@
     return (scalar(ref[base + 7 : base + 8, :]) + 127) // 128
 
 
-def spread_kernel(count_ref, span_ref, list_ref, below_ref, above_ref, grid_ref, a_ref, b_ref, wx_ref):
+def spread_kernel(count_ref, span_ref, list_ref, grid_ref, a_ref, b_ref, wx_ref):
     for j in range(6):
         grid_ref[j] = jnp.zeros(grid_ref.shape[1:], F32)
     spread_list(list_ref, (count_ref[0] + 3) // 4, span_ref, grid_ref, a_ref, b_ref, wx_ref)
-    spread_edges(
-        [
-            (below_ref, 8 * CX, 0, tiles_of(below_ref, 8 * CX), 0, -1),
-            (above_ref, 16 * CX, 0, tiles_of(above_ref, 16 * CX), 0, 1),
-        ],
-        grid_ref,
-    )
-
-
-def spread(count, span, markers, below, above):
+
+
+def spread(count, span, markers):
     return pl.pallas_call(
         spread_kernel,
         out_shape=jax.ShapeDtypeStruct((6, PLANES + WINDOW, ROWS, 128), F32),
-        in_specs=[SMEM, SMEM] + [VMEM] * 3,
+        in_specs=[SMEM, SMEM, VMEM],
         out_specs=VMEM,
         compiler_params=pltpu.CompilerParams(vmem_limit_bytes=16 * MIB),
         scratch_shapes=[
@@ -424,36 +417,84 @@
         ],
         cost_estimate=pl.CostEstimate(flops=6_000_000_000, bytes_accessed=6_000_000, transcendentals=0),
         name="spread",
-    )(count, span, markers, below, above)
+    )(count, span, markers)
+
+
+DEPTH = 128 * (GROUPS + REACH)
+
+
+def advance(g, old, grid_ref, fresh_ref, ut_ref, owned):
+    planes = pl.ds(3 * g, 3)
+    for h in range(2):
+        half_over = 0.5 / old(6 + h)
+        for c in range(3):
+            j = 2 * c + h
+            value = old(j) + grid_ref[j, planes] * half_over
+            for i, x in owned:
+                fresh_ref[j, x] = value[i, :CY]
+            flat = jnp.concatenate([value.reshape(3 * ROWS, 128), jnp.zeros((8, 128), F32)], axis=0)
+            high, low = split(flat.T)
+            rows = slice(128 * j, 128 * j + 128)
+            ut_ref[rows, pl.ds(pl.multiple_of(128 * g, 128), 128)] = high
+            ut_ref[rows, pl.ds(pl.multiple_of(DEPTH + 128 * g, 128), 128)] = low
+
+
+def own_plane(u_ref, rho_ref, rim_ref, j, e):
+    lanes = slice(128 * (j % 2), 128 * (j % 2) + 128)
+    inner = u_ref[j // 2, e - 1, :, lanes] if j < 6 else rho_ref[e - 1, :, lanes]
+    return jnp.concatenate([inner, rim_ref[j, e]], axis=0)
+
+
+def middle_kernel(u_ref, rho_ref, below_ref, above_ref, grid_in, grid_ref, fresh_ref, ut_ref, rim_ref):
+    spread_edges(
+        [
+            (below_ref, 8 * CX, 0, tiles_of(below_ref, 8 * CX), 0, -1),
+            (above_ref, 16 * CX, 0, tiles_of(above_ref, 16 * CX), 0, 1),
+        ],
+        grid_ref,
+    )
+    for j in range(8):
+        rim_ref[j] = jnp.full((PLANES, 8, 128), 0.0 if j < 6 else 1.0, F32)
+        rim_ref[j, 1:33, 7, :] = below_ref[CX * j : CX * (j + 1), :]
+        rim_ref[j, 1:33, 0, :] = above_ref[2 * CX * j : 2 * CX * j + CX, :]
+        rim_ref[j, 1:33, 1, :] = above_ref[2 * CX * j + CX : 2 * CX * (j + 1), :]
+    for part in range(2):
+        start = DEPTH * part + 128 * GROUPS
+        ut_ref[:, start : start + 128 * REACH] = jnp.zeros((768, 128 * REACH), BF16)
+
+    def group(g, carry):
+        def old(j):
+            return jnp.stack([own_plane(u_ref, rho_ref, rim_ref, j, 3 * g + i) for i in range(3)])
+
+        advance(g, old, grid_ref, fresh_ref, ut_ref, [(i, 3 * g + i - 1) for i in range(3)])
+        return carry
+
+    lax.fori_loop(1, 10, group, 0)
+
+
+def middle(u_old, density, below, above, grid):
+    return pl.pallas_call(
+        middle_kernel,
+        out_shape=[
+            jax.ShapeDtypeStruct(grid.shape, F32),
+            jax.ShapeDtypeStruct((6, CX, CY, 128), F32),
+            jax.ShapeDtypeStruct((768, 2 * DEPTH), BF16),
+            jax.ShapeDtypeStruct((8, PLANES, 8, 128), F32),
+        ],
+        in_specs=[VMEM] * 5,
+        out_specs=[VMEM] * 4,
+        input_output_aliases={4: 0},
+        compiler_params=pltpu.CompilerParams(vmem_limit_bytes=24 * MIB),
+        cost_estimate=pl.CostEstimate(flops=6_000_000_000, bytes_accessed=6_000_000, transcendentals=0),
+        name="middle",
+    )(u_old, density, below, above, grid)
 
 
 def finish_kernel(
-    count_ref, span_ref, list_ref, pos_ref, u_ref, rho_ref, below_ref, above_ref, left_ref, right_ref, force_ref,
-    out_ref, vel_ref, grid_ref, state, ut_ref, a_ref, wx_ref, sorted_ref, sems, out_sem,
+    count_ref, span_ref, list_ref, pos_ref, u_ref, rho_ref, rim_ref, left_ref, right_ref, grid_in, fresh_in, ut_in,
+    out_ref, vel_ref, grid_ref, fresh_ref, ut_ref, a_ref, wx_ref, sorted_ref, out_sem,
 ):
     count = count_ref[0]
-    copies = []
-    for c in range(4):
-        for h in range(2):
-            lanes = pl.ds(128 * h, 128)
-            src = u_ref.at[c, :, :, lanes] if c < 3 else rho_ref.at[:, :, lanes]
-            copies.append(
-                pltpu.make_async_copy(
-                    src, state.at[2 * c + h, pl.ds(1, CX), pl.ds(0, CY), :], sems.at[2 * c + h]
-                )
-            )
-    for copy in copies:
-        copy.start()
-    for j in range(8):
-        fill = 0.0 if j < 6 else 1.0
-        state[j, :, 32:40, :] = jnp.full((PLANES, 8, 128), fill, F32)
-        state[j, 35, 0:32, :] = jnp.full((32, 128), fill, F32)
-        state[j, 0] = left_ref[ROWS * j : ROWS * (j + 1), :]
-        state[j, 33] = right_ref[2 * ROWS * j : 2 * ROWS * j + ROWS, :]
-        state[j, 34] = right_ref[2 * ROWS * j + ROWS : 2 * ROWS * (j + 1), :]
-        state[j, 1:33, 39, :] = below_ref[CX * j : CX * (j + 1), :]
-        state[j, 1:33, 32, :] = above_ref[2 * CX * j : 2 * CX * j + CX, :]
-        state[j, 1:33, 33, :] = above_ref[2 * CX * j + CX : 2 * CX * (j + 1), :]
     lo, ro = 8 * ROWS, 16 * ROWS
     ends = [
         scalar(left_ref[lo + 15 : lo + 16, :]) // 128, (scalar(left_ref[lo + 23 : lo + 24, :]) + 127) // 128,
@@ -470,45 +511,32 @@
         ],
         grid_ref,
     )
-    for copy in copies:
-        copy.wait()
-
-    def group(g, carry):
-        e = 3 * g
-        planes = pl.ds(e, 3)
-        for h in range(2):
-            half_over = 0.5 / state[6 + h, planes]
-            for c in range(3):
-                j = 2 * c + h
-                value = state[j, planes] + grid_ref[j, planes] * half_over
-                state[j, planes] = value
-                flat = jnp.concatenate([value.reshape(3 * ROWS, 128), jnp.zeros((8, 128), F32)], axis=0)
-                high, low = split(flat.T)
-                rows = slice(128 * j, 128 * j + 128)
-                ut_ref[rows, pl.ds(pl.multiple_of(128 * g, 128), 128)] = high
-                ut_ref[rows, pl.ds(pl.multiple_of(128 * (GROUPS + REACH + g), 128), 128)] = low
-        return carry
-
-    lax.fori_loop(0, GROUPS, group, 0)
+
+    def plane(j, e):
+        if e == 0:
+            return left_ref[ROWS * j : ROWS * (j + 1), :]
+        if e in (33, 34):
+            return right_ref[ROWS * (2 * j + e - 33) : ROWS * (2 * j + e - 32), :]
+        if e == 35:
+            return jnp.full((ROWS, 128), 0.0 if j < 6 else 1.0, F32)
+        return own_plane(u_ref, rho_ref, rim_ref, j, e)
+
+    for g in (0, 10, 11):
+        advance(
+            g, lambda j, g=g: jnp.stack([plane(j, 3 * g + i) for i in range(3)]), grid_ref, fresh_ref, ut_ref,
+            [(i, 3 * g + i - 1) for i in range(3) if 1 <= 3 * g + i <= CX],
+        )
     outs = []
     for c in range(3):
         for h in range(2):
             outs.append(
                 pltpu.make_async_copy(
-                    state.at[2 * c + h, pl.ds(1, CX), pl.ds(0, CY), :],
-                    out_ref.at[c, :, :, pl.ds(128 * h, 128)],
-                    out_sem.at[2 * c + h],
+                    fresh_ref.at[2 * c + h], out_ref.at[c, :, :, pl.ds(128 * h, 128)], out_sem.at[2 * c + h]
                 )
             )
     for copy in outs:
         copy.start()
-
-    depth = 128 * (GROUPS + REACH)
-    for part in range(2):
-        start = depth * part + 128 * GROUPS
-        ut_ref[:, start : start + 128 * REACH] = jnp.zeros((768, 128 * REACH), BF16)
     sorted_ref[...] = jnp.zeros(sorted_ref.shape, F32)
-
     wide = 128 * REACH
 
     def tables(j):
@@ -523,7 +551,7 @@
             a_ref[k, 128 * i : 128 * i + 128, :] = high
             a_ref[k, 128 * (REACH + i) : 128 * (REACH + i) + 128, :] = low
         ut_high = ut_ref[:, pl.ds(pl.multiple_of(128 * g, 128), wide)]
-        ut_low = ut_ref[:, pl.ds(pl.multiple_of(depth + 128 * g, 128), wide)]
+        ut_low = ut_ref[:, pl.ds(pl.multiple_of(DEPTH + 128 * g, 128), wide)]
         high, low = a_ref[k, :wide, :], a_ref[k, wide:, :]
         picked = (
             jnp.dot(ut_high, high, preferred_element_type=F32)
@@ -575,7 +603,7 @@
         copy.wait()
 
 
-def finish(count, span, markers, pos, u_old, density, below, above, left, right, grid):
+def finish(count, span, markers, pos, u_old, density, rim, left, right, grid, fresh, ut):
     slots = pos.shape[0]
     return pl.pallas_call(
         finish_kernel,
@@ -583,23 +611,22 @@
             jax.ShapeDtypeStruct(u_old.shape, F32),
             jax.ShapeDtypeStruct((3, slots, 128), F32),
             jax.ShapeDtypeStruct(grid.shape, F32),
-        ],
-        input_output_aliases={10: 2},
-        in_specs=[SMEM, SMEM, VMEM, VMEM] + [HBM, HBM] + [VMEM] * 5,
-        out_specs=[HBM, VMEM, VMEM],
-        compiler_params=pltpu.CompilerParams(vmem_limit_bytes=36 * MIB),
+            jax.ShapeDtypeStruct(fresh.shape, F32),
+            jax.ShapeDtypeStruct(ut.shape, BF16),
+        ],
+        in_specs=[SMEM, SMEM] + [VMEM] * 10,
+        out_specs=[HBM] + [VMEM] * 4,
+        input_output_aliases={9: 2, 10: 3, 11: 4},
+        compiler_params=pltpu.CompilerParams(vmem_limit_bytes=24 * MIB),
         scratch_shapes=[
-            pltpu.VMEM((8, PLANES, ROWS, 128), F32),
-            pltpu.VMEM((768, 2 * 128 * (GROUPS + REACH)), BF16),
             pltpu.VMEM((2, 2 * 128 * REACH, 256), BF16),
             pltpu.VMEM((2, 16, 256), F32),
             pltpu.VMEM((8, 128 * slots), F32),
-            pltpu.SemaphoreType.DMA((9,)),
             pltpu.SemaphoreType.DMA((6,)),
         ],
         cost_estimate=pl.CostEstimate(flops=6_000_000_000, bytes_accessed=12_000_000, transcendentals=0),
         name="finish",
-    )(count, span, markers, pos, u_old, density, below, above, left, right, grid)[:2]
+    )(count, span, markers, pos, u_old, density, rim, left, right, grid, fresh, ut)[:2]
 
 
 def shift(value, axis, steps):
@@ -613,11 +640,12 @@
     below = shift(to_next, "gy", 1)
     above = shift(to_previous, "gy", -1)
     markers, pos, span = sort(tile_count, payload)
+    grid = spread(tile_count, span, markers)
     to_next, to_previous = pack_x(u_old, density, below, above, markers)
     left = shift(to_next, "gx", 1)
     right = shift(to_previous, "gx", -1)
-    grid = spread(tile_count, span, markers, below, above)
-    return finish(tile_count, span, markers, pos, u_old, density, below, above, left, right, grid)[:2]
+    grid, fresh, ut, rim = middle(u_old, density, below, above, grid)
+    return finish(tile_count, span, markers, pos, u_old, density, rim, left, right, grid, fresh, ut)
 
 
 def solution(mesh):

time: 47.5 us -> 45.3 us (0.954)
  the two profiles are of different devices: /device:TPU:25 before, /device:TPU:13 now
where the time goes in v2:
time: 45.3 us; the launch traced here: 45.2 us
  Pallas kernels  26.1 us (58%)
  starting transfers between devices  11.8 us (26%)
  waiting for transfers between devices  4.78 us (11%)
  between operations  1.53 us (3%)
  local copies, waits for them, and re-layouts  0.92 us (2%)
    ppermute x4, starting transfers between devices, shift(): lax.ppermute(value, axis, [(i, (i + steps) % count) for i in range(count)])  11.8 us
    pallas_call x1, Pallas kernels, finish(): pl.pallas_call(finish_kernel, out_shape=[jax.ShapeDtypeStruct(u_old.shape...  10.1 us
    pallas_call x1, Pallas kernels, spread(): pl.pallas_call(spread_kernel, out_shape=jax.ShapeDtypeStruct((6, PLANES +...  5.52 us
    ppermute x4, waiting for transfers between devices, shift(): lax.ppermute(value, axis, [(i, (i + steps) % count) for i in range(count)])  4.78 us
    pallas_call x1, Pallas kernels, middle(): pl.pallas_call(middle_kernel, out_shape=[jax.ShapeDtypeStruct(grid.shape,...  3.82 us
    pallas_call x1, Pallas kernels, pack_y(): pl.pallas_call(pack_y_kernel, out_shape=[jax.ShapeDtypeStruct((8 * CX + L...  3.63 us
    pallas_call x1, Pallas kernels, sort(): pl.pallas_call(sort_kernel, out_shape=[jax.ShapeDtypeStruct((LIST, 128),...  2.59 us
    unnamed x6, local copies, waits for them, and re-layouts  0.92 us
  transfers between devices with their start and end apart: 4, of which 2 were waited for; matrix products, arithmetic and copies ran while one was open for 0% of the time, Pallas kernels for 26%

profile of v2, /device:TPU:13, one launch (start us, length us, event | category | flops | bytes accessed | tf_op | source)
XLA Modules:
  0.0 45.2 jit_solution(11886629380975898470)
XLA Ops:
  1.3 3.6 %pack_y.1 = (f32[384,128]{1,0:T(8,128)}, f32[640,128]{1,0:T(8,128)}, f32[16,2048]{1,0:T(8,128)}) custom-call(s32[1]{0:T(128)S(6)} %copy.18.count_ref, f32[3,16,128]{2,1,0:T(8,128)} %off_hbm.1, f32[3,16,128]{2,1,0:T(8,128)} %force_hbm.1, s32[16,128]{1,0:T(8,128)} %bx_hbm.1, s32[16,128]{1,0:T(8,128)} %by_hbm.1, s32[16,128]{1,0:T(8,128)} %bz_hbm.1, ...), custom_call_target="tpu_custom_call" | custom-call | tf_op jit(solution)/shard_map/pack_y/pallas_call | solution.py:196
  4.9 1.7 %collective-permute-start = (f32[384,128]{1,0:T(8,128)}, f32[384,128]{1,0:T(8,128)S(1)}, u32[]{:S(2)}, u32[]{:S(2)}) collective-permute-start(f32[384,128]{1,0:T(8,128)} %get-tuple-element.20), channel_id=1, source_target_pairs={{0,1},{1,2},{2,3},{3,4},{4,5},{5,6},{6,7},{7,8},{8,9},{9,10},{10,1... | collective-permute-start | bytes 589832 | tf_op jit(solution)/shard_map/ppermute | solution.py:634
  6.6 4.7 %collective-permute-start.1 = (f32[640,128]{1,0:T(8,128)}, f32[640,128]{1,0:T(8,128)S(1)}, u32[]{:S(2)}, u32[]{:S(2)}) collective-permute-start(f32[640,128]{1,0:T(8,128)} %get-tuple-element.21), channel_id=1, source_target_pairs={{0,15},{1,0},{2,1},{3,2},{4,3},{5,4},{6,5},{7,6},{8,7},{9,8},{10,9... | collective-permute-start | bytes 983048 | tf_op jit(solution)/shard_map/ppermute | solution.py:634
  11.3 0.0 copy-start.2
  11.3 0.9 %copy-done.2 = f32[16,2048]{1,0:T(8,128)S(1)} copy-done((f32[16,2048]{1,0:T(8,128)S(1)}, f32[16,2048]{1,0:T(8,128)}, u32[]{:S(2)}) %copy-start.2) | copy-done | bytes 131096
  12.2 2.6 %sort.1 = (f32[128,128]{1,0:T(8,128)S(1)}, f32[16,128]{1,0:T(8,128)S(1)}, s32[16]{0:T(128)S(1)}) custom-call(s32[1]{0:T(128)S(6)} %copy.18.count_ref, f32[16,2048]{1,0:T(8,128)S(1)} %copy-done.2), custom_call_target="tpu_custom_call" | custom-call | flops 3000000000 | bytes 400000 | tf_op jit(solution)/shard_map/sort/pallas_call | solution.py:253
  14.8 0.0 copy-start
  14.8 0.0 copy-start.1
  14.8 5.5 %spread.1.grid_in = f32[6,45,40,128]{3,2,1,0:T(8,128)S(1)} custom-call(s32[1]{0:T(128)S(6)} %copy.18.count_ref, s32[16]{0:T(128)S(1)} %get-tuple-element.17.span_ref, f32[128,128]{1,0:T(8,128)S(1)} %get-tuple-element.18.list_ref), custom_call_target="tpu_custom_call" | custom-call | flops 6000000000 | bytes 6000000 | tf_op jit(solution)/shard_map/spread/pallas_call | solution.py:407
  20.3 0.0 collective-permute-done.below_ref
  20.4 0.0 collective-permute-done.1.above_ref
  20.4 0.0 copy-done
  20.4 0.0 copy-done.1
  20.4 0.4 pack_x.1
  20.8 5.5 %collective-permute-start.2 = (f32[704,128]{1,0:T(8,128)S(1)}, f32[704,128]{1,0:T(8,128)S(1)}, u32[]{:S(2)}, u32[]{:S(2)}) collective-permute-start(f32[704,128]{1,0:T(8,128)S(1)} %get-tuple-element.23), channel_id=1, source_target_pairs={{0,16},{16,32},{32,48},{48,64},{64,80},{80,96},{96,112},{112,128},... | collective-permute-start | bytes 1081352 | tf_op jit(solution)/shard_map/ppermute | solution.py:634
  26.3 0.0 collective-permute-start.3
  26.3 3.8 %middle.1 = (f32[6,45,40,128]{3,2,1,0:T(8,128)S(1)}, f32[6,32,32,128]{3,2,1,0:T(8,128)S(1)}, bf16[768,4096]{1,0:T(8,128)(2,1)S(1)}, f32[8,36,8,128]{3,2,1,0:T(8,128)S(1)}) custom-call(f32[3,32,32,256]{3,2,1,0:T(8,128)S(1)} %copy-done, f32[32,32,256]{2,1,0:T(8,128)S(1)} %copy-done.1, ...), custom_call_target="tpu_custom_call", output_to_operand_aliasing={{0}: (4, {})} | custom-call | flops 6000000000 | bytes 6000000 | tf_op jit(solution)/shard_map/middle/pallas_call | solution.py:476
  30.1 0.5 %collective-permute-done.2.left_ref = f32[704,128]{1,0:T(8,128)S(1)} collective-permute-done((f32[704,128]{1,0:T(8,128)S(1)}, f32[704,128]{1,0:T(8,128)S(1)}, u32[]{:S(2)}, u32[]{:S(2)}) %collective-permute-start.2) | collective-permute-done | bytes 360480 | tf_op jit(solution)/shard_map/ppermute | solution.py:634
  30.7 4.2 %collective-permute-done.3.right_ref = f32[1024,128]{1,0:T(8,128)S(1)} collective-permute-done((f32[1024,128]{1,0:T(8,128)S(1)}, f32[1024,128]{1,0:T(8,128)S(1)}, u32[]{:S(2)}, u32[]{:S(2)}) %collective-permute-start.3) | collective-permute-done | bytes 524320 | tf_op jit(solution)/shard_map/ppermute | solution.py:634
  34.9 10.1 %finish.1 = (f32[3,32,32,256]{3,2,1,0:T(8,128)}, f32[3,16,128]{2,1,0:T(8,128)}, f32[6,45,40,128]{3,2,1,0:T(8,128)S(1)}, f32[6,32,32,128]{3,2,1,0:T(8,128)S(1)}, bf16[768,4096]{1,0:T(8,128)(2,1)S(1)}) custom-call(s32[1]{0:T(128)S(6)} %copy.18.count_ref, ...), custom_call_target="tpu_custom_call", output_to_operand_aliasing={{2}: (9, {}), {3}: (10, {}), {4}: (11, {})} | custom-call | flops 6000000000 | bytes 12000000 | tf_op jit(solution)/shard_map/finish/pallas_call | solution.py:608
Async XLA Ops:
  4.9 15.4 %collective-permute-start = (f32[384,128]{1,0:T(8,128)}, f32[384,128]{1,0:T(8,128)S(1)}, u32[]{:S(2)}, u32[]{:S(2)}) collective-permute-start(f32[384,128]{1,0:T(8,128)} %get-tuple-element.20), channel_id=1, source_target_pairs={{0,1},{1,2},{2,3},{3,4},{4,5},{5,6},{6,7},{7,8},{8,9},{9,10},{10,1... | collective-permute-start | bytes 589832 | tf_op jit(solution)/shard_map/ppermute | solution.py:634
  6.6 13.7 %collective-permute-start.1 = (f32[640,128]{1,0:T(8,128)}, f32[640,128]{1,0:T(8,128)S(1)}, u32[]{:S(2)}, u32[]{:S(2)}) collective-permute-start(f32[640,128]{1,0:T(8,128)} %get-tuple-element.21), channel_id=1, source_target_pairs={{0,15},{1,0},{2,1},{3,2},{4,3},{5,4},{6,5},{7,6},{8,7},{9,8},{10,9... | collective-permute-start | bytes 983048 | tf_op jit(solution)/shard_map/ppermute | solution.py:634
  11.3 0.9 %copy-start.2 = (f32[16,2048]{1,0:T(8,128)S(1)}, f32[16,2048]{1,0:T(8,128)}, u32[]{:S(2)}) copy-start(f32[16,2048]{1,0:T(8,128)} %get-tuple-element.16.pay_ref) | copy-start | bytes 393220
  14.8 5.6 %copy-start = (f32[3,32,32,256]{3,2,1,0:T(8,128)S(1)}, f32[3,32,32,256]{3,2,1,0:T(8,128)}, u32[]{:S(2)}) copy-start(f32[3,32,32,256]{3,2,1,0:T(8,128)} %u_ref.7) | copy-start | bytes 9437188
  14.8 5.6 %copy-start.1 = (f32[32,32,256]{2,1,0:T(8,128)S(1)}, f32[32,32,256]{2,1,0:T(8,128)}, u32[]{:S(2)}) copy-start(f32[32,32,256]{2,1,0:T(8,128)} %rho_ref.7) | copy-start | bytes 3145732
  20.8 9.8 %collective-permute-start.2 = (f32[704,128]{1,0:T(8,128)S(1)}, f32[704,128]{1,0:T(8,128)S(1)}, u32[]{:S(2)}, u32[]{:S(2)}) collective-permute-start(f32[704,128]{1,0:T(8,128)S(1)} %get-tuple-element.23), channel_id=1, source_target_pairs={{0,16},{16,32},{32,48},{48,64},{64,80},{80,96},{96,112},{112,128},... | collective-permute-start | bytes 1081352 | tf_op jit(solution)/shard_map/ppermute | solution.py:634
  26.3 8.6 %collective-permute-start.3 = (f32[1024,128]{1,0:T(8,128)S(1)}, f32[1024,128]{1,0:T(8,128)S(1)}, u32[]{:S(2)}, u32[]{:S(2)}) collective-permute-start(f32[1024,128]{1,0:T(8,128)S(1)} %get-tuple-element.24), channel_id=1, source_target_pairs={{0,240},{16,0},{32,16},{48,32},{64,48},{80,64},{96,80},{112,96},{1... | collective-permute-start | bytes 1572872 | tf_op jit(solution)/shard_map/ppermute | solution.py:634

commit v3 on v2

v3 whole, which is shorter than its diff:
```python
import jax
import jax.numpy as jnp
from jax import lax
from jax.experimental import pallas as pl
from jax.experimental.pallas import tpu as pltpu
from jax.sharding import PartitionSpec as P


CX, CY, ROWS, PLANES = 32, 32, 40, 36
GROUPS = 12
WINDOW = 9
TALL = 368
REACH = 4
TILES = 16
DEEP, COUNTS = 8 * TILES, 9 * TILES
LIST = 9 * TILES + 8
PATCH = 6 * 24
F32, BF16 = jnp.float32, jnp.bfloat16
VMEM = pl.BlockSpec(memory_space=pltpu.VMEM)
SMEM = pl.BlockSpec(memory_space=pltpu.SMEM)
HBM = pl.BlockSpec(memory_space=pltpu.MemorySpace.HBM)
MIB = 2**20


def stencil(frac):
    root = jnp.sqrt(1.0 + 4.0 * frac - 4.0 * frac * frac)
    return [
        (3.0 - 2.0 * frac - root) / 8.0,
        (3.0 - 2.0 * frac + root) / 8.0,
        (1.0 + 2.0 * frac + root) / 8.0,
        (1.0 + 2.0 * frac - root) / 8.0,
    ]


def spread_four(rows, targets, weights):
    row = lax.broadcasted_iota(jnp.int32, (rows, targets[0].shape[1]), 0)
    total = jnp.zeros(row.shape, F32)
    for target, weight in zip(targets, weights):
        total = jnp.where(row == target, weight, total)
    return total


def split(value):
    high = value.astype(BF16)
    return high, (value - high.astype(F32)).astype(BF16)


def split3(value):
    high, rest = value.astype(BF16), value
    parts = [high]
    for _ in range(2):
        rest = rest - parts[-1].astype(F32)
        parts.append(rest.astype(BF16))
    return parts


def x_table(rows, base_x, first, weights):
    return spread_four(rows, [base_x + (a - first) for a in range(4)], weights)


def y_table(base_y, weights):
    targets = []
    for b in range(4):
        y = base_y + (b - 1)
        targets.append(jnp.where((y < -1) | (y > CY + 1), -1, jnp.where(y < 0, ROWS - 1, y)))
    return spread_four(ROWS, targets, weights)


def one_row(base, target, weights):
    total = jnp.zeros(base.shape, F32)
    for shift, weight in enumerate(weights):
        total = jnp.where(base + (shift - 1) == target, weight, total)
    return total


def z_table(base_z, weights):
    return spread_four(256, [(base_z + c - 1) & 255 for c in range(4)], weights)


def fill_payload(pay_ref, off_ref, force_ref, bx_ref, by_ref, bz_ref):
    for t in range(TILES):
        lanes = slice(128 * t, 128 * t + 128)
        for c in range(3):
            pay_ref[c : c + 1, lanes] = off_ref[c, t : t + 1, :]
            pay_ref[3 + c : 4 + c, lanes] = force_ref[c, t : t + 1, :]
        pay_ref[6:7, lanes] = bx_ref[t : t + 1, :].astype(F32)
        pay_ref[7:8, lanes] = by_ref[t : t + 1, :].astype(F32)
        pay_ref[14:15, lanes] = bz_ref[t : t + 1, :].astype(F32)
        pay_ref[15:16, lanes] = jnp.ones((1, 128), F32)


def payload_of(pay_ref):
    first, second, third = split3(pay_ref[0:8, :])
    row8 = lax.broadcasted_iota(jnp.int32, first.shape, 0)
    second = jnp.where(row8 < 6, second.astype(F32), pay_ref[8:16, :])
    return jnp.concatenate([first.astype(F32), second, third.astype(F32)], axis=0).astype(BF16)


def columns_of(rows, col_ref):
    columns = jnp.concatenate([rows, jnp.zeros((128 - TILES, 128), F32)], axis=0).T
    for t in range(TILES):
        col_ref[128 * t : 128 * t + 128, :] = jnp.broadcast_to(columns[:, t : t + 1], (128, 128))


def gather(payload, col_ref, j, start, list_ref, base):
    lane = lax.broadcasted_iota(jnp.int32, (128 * TILES, 128), 1).astype(F32)
    here = col_ref[...] - (start + 256 * j).astype(F32)
    pick = jnp.concatenate([jnp.where(here == lane + 128.0 * h, 1.0, 0.0).astype(BF16) for h in range(2)], axis=1)
    parts = jnp.dot(payload, pick, preferred_element_type=F32)
    row = lax.broadcasted_iota(jnp.int32, (8, 256), 0)
    fields = jnp.where(row < 6, parts[0:8] + parts[8:16] + parts[16:24], parts[0:8])
    for h in range(2):
        lanes = slice(128 * h, 128 * h + 128)
        list_ref[pl.ds(pl.multiple_of(base + 16 * j, 8) + 8 * h, 8), :] = fields[:, lanes]
        list_ref[pl.ds(base + DEEP + 2 * j + h, 1), :] = parts[14:15, lanes]
    return parts


def running():
    i0 = lax.broadcasted_iota(jnp.int32, (128, 256), 0)
    i1 = lax.broadcasted_iota(jnp.int32, (128, 256), 1)
    return jnp.where(i0 <= i1, 1.0, 0.0).astype(BF16)


def scalar(row):
    return jnp.max(row).astype(jnp.int32)


def decode(block, deep):
    weights = [stencil(block[c : c + 1]) for c in range(3)]
    bases = [row.astype(jnp.int32) for row in (block[6:7], block[7:8], deep)]
    return weights, [block[3 + c : 4 + c] for c in range(3)], bases


def chunk_of(list_ref, j):
    rows = pl.multiple_of(16 * j, 8)
    block = jnp.concatenate([list_ref[pl.ds(rows, 8), :], list_ref[pl.ds(rows + 8, 8), :]], axis=1)
    deep = jnp.concatenate([list_ref[pl.ds(DEEP + 2 * j + h, 1), :] for h in range(2)], axis=1)
    return decode(block, deep)


def pack_y_kernel(
    count_ref, off_hbm, force_hbm, bx_hbm, by_hbm, bz_hbm, u_ref, rho_ref, yn_ref, yp_ref, pay_ref,
    off_ref, force_ref, bx_ref, by_ref, bz_ref, slab, col_ref, sems,
):
    loads = [
        pltpu.make_async_copy(src, dst, sems.at[2, n])
        for n, (src, dst) in enumerate(
            zip((by_hbm, bx_hbm, bz_hbm, off_hbm, force_hbm), (by_ref, bx_ref, bz_ref, off_ref, force_ref))
        )
    ]
    for load in loads:
        load.start()
    copies = []
    for c in range(4):
        for h in range(2):
            j, lanes = 2 * c + h, pl.ds(128 * h, 128)
            for n in range(2):
                ys = pl.ds((CY - 8) * n, 8)
                src = u_ref.at[c, :, ys, lanes] if c < 3 else rho_ref.at[:, ys, lanes]
                copies.append(pltpu.make_async_copy(src, slab.at[n, j], sems.at[n, j]))
    for copy in copies:
        copy.start()
    count = count_ref[0]
    for load in loads:
        load.wait()
    tile = lax.broadcasted_iota(jnp.int32, (TILES, 128), 0)
    y = jnp.where(tile < count, by_ref[...], CY // 2)
    low, high = (y < 3).astype(F32), (y > CY - 4).astype(F32)
    counts = jnp.dot(jnp.concatenate([low, high], axis=0).astype(BF16), running(), preferred_element_type=F32)
    below = lax.broadcasted_iota(jnp.int32, (2 * TILES, 2 * TILES), 0)
    left = lax.broadcasted_iota(jnp.int32, (2 * TILES, 2 * TILES), 1)
    earlier = jnp.where((left < below) & ((left < TILES) == (below < TILES)), 1.0, 0.0).astype(BF16)
    before = jnp.dot(earlier, counts[:, 128:].astype(BF16), preferred_element_type=F32)
    place = counts[:, :128] + before - 1.0
    columns_of(low * (place[:TILES] + 1.0) + high * (place[TILES:] + 4097.0) - 1.0, col_ref)
    fill_payload(pay_ref, off_ref, force_ref, bx_ref, by_ref, bz_ref)
    payload = payload_of(pay_ref)
    ends = before + counts[:, 128:]
    for n, (ref, base, start) in enumerate(((yp_ref, 16 * CX, 0), (yn_ref, 8 * CX, 4096))):
        end = ends[TILES * n + TILES - 1 : TILES * n + TILES]
        size = scalar(end)

        def chunk(j, carry, ref=ref, base=base, start=start):
            gather(payload, col_ref, j, start, ref, base)
            return carry

        lax.fori_loop(0, jnp.maximum((size + 255) // 256, 1), chunk, 0)
        ref[base + COUNTS : base + COUNTS + 1, :] = end
    for copy in copies:
        copy.wait()
    for j in range(8):
        for r in range(2):
            yp_ref[(2 * j + r) * CX : (2 * j + r + 1) * CX, :] = slab[0, j, :, r, :]
        yn_ref[j * CX : (j + 1) * CX, :] = slab[1, j, :, 7, :]


def pack_y(count, arrays, u_old, density):
    return pl.pallas_call(
        pack_y_kernel,
        out_shape=[
            jax.ShapeDtypeStruct((8 * CX + LIST, 128), F32),
            jax.ShapeDtypeStruct((16 * CX + LIST, 128), F32),
            jax.ShapeDtypeStruct((16, 128 * TILES), F32),
        ],
        in_specs=[SMEM] + [HBM] * 7,
        out_specs=[VMEM] * 3,
        scratch_shapes=[
            pltpu.VMEM((3, TILES, 128), F32),
            pltpu.VMEM((3, TILES, 128), F32),
            pltpu.VMEM((TILES, 128), jnp.int32),
            pltpu.VMEM((TILES, 128), jnp.int32),
            pltpu.VMEM((TILES, 128), jnp.int32),
            pltpu.VMEM((2, 8, CX, 8, 128), F32),
            pltpu.VMEM((128 * TILES, 128), F32),
            pltpu.SemaphoreType.DMA((3, 8)),
        ],
        name="pack_y",
    )(count, *arrays, u_old, density)


def sort_kernel(count_ref, pay_ref, list_ref, pos_ref, span_ref, col_ref):
    count = count_ref[0]
    list_ref[...] = jnp.zeros(list_ref.shape, F32)
    key_row = lax.broadcasted_iota(jnp.int32, (CX, 128), 0)
    keys = [
        jnp.where(t < count, pay_ref[6:7, 128 * t : 128 * t + 128].astype(jnp.int32), 2 * CX) for t in range(TILES)
    ]
    same = [(key_row == k).astype(F32) for k in keys]
    less = [(k < key_row).astype(F32) for k in keys]
    counts = jnp.dot(jnp.concatenate(same, axis=0).astype(BF16), running(), preferred_element_type=F32)
    smaller = jnp.dot(sum(less).astype(BF16), jnp.ones((128, 128), BF16), preferred_element_type=F32)
    before = smaller
    for t in range(TILES):
        part = counts[CX * t : CX * t + CX]
        pos_ref[t : t + 1, :] = jnp.sum(same[t] * (part[:, :128] + before), axis=0, keepdims=True) - 1.0
        before = before + part[:, 128:]
    columns_of(pos_ref[...], col_ref)
    payload = payload_of(pay_ref)

    def chunks(p, carry):
        for j in (2 * p, 2 * p + 1):
            parts = gather(payload, col_ref, j, 0, list_ref, 0)
            there = parts[15:16] > 0.5
            span_ref[2 * j] = jnp.min(jnp.where(there, parts[6:7], CX - 1.0)).astype(jnp.int32)
            span_ref[2 * j + 1] = scalar(jnp.where(there, parts[6:7], 0.0))
        return carry

    lax.fori_loop(0, (count + 3) // 4, chunks, 0)
    list_ref[COUNTS : COUNTS + 1, :] = smaller[3:4]
    list_ref[COUNTS + 1 : COUNTS + 2, :] = smaller[CX - 3 : CX - 2]
    list_ref[COUNTS + 2 : COUNTS + 3, :] = jnp.full((1, 128), (128 * count).astype(F32))


def sort(count, payload):
    return pl.pallas_call(
        sort_kernel,
        out_shape=[
            jax.ShapeDtypeStruct((LIST, 128), F32),
            jax.ShapeDtypeStruct((TILES, 128), F32),
            jax.ShapeDtypeStruct((TILES,), jnp.int32),
        ],
        in_specs=[SMEM, VMEM],
        out_specs=[VMEM, VMEM, SMEM],
        compiler_params=pltpu.CompilerParams(vmem_limit_bytes=8 * MIB),
        scratch_shapes=[pltpu.VMEM((128 * TILES, 128), F32)],
        cost_estimate=pl.CostEstimate(flops=3_000_000_000, bytes_accessed=400_000, transcendentals=0),
        name="sort",
    )(count, payload)


def spread_list(list_ref, begin, end, span_ref, grid_ref, a_ref, b_ref, wx_ref):
    def tables(j, k):
        (weight_x, weight_y, weight_z), forces, (base_x, base_y, base_z) = chunk_of(list_ref, j)
        wy, wz = y_table(base_y, weight_y), z_table(base_z, weight_z)
        for c in range(3):
            high, low = split(wz * forces[c])
            b_ref[k, 0, 256 * c : 256 * c + 256, :] = high
            b_ref[k, 1, 256 * c : 256 * c + 256, :] = low
        return weight_x, base_x, wy

    def window(first, weight_x, base_x, wy, k):
        wx_ref[k] = x_table(16, base_x, first, weight_x)
        rows = [wx_ref[k, e : e + 1, :] * wy for e in range(WINDOW)]
        high, low = split(jnp.concatenate(rows + [jnp.zeros((TALL - WINDOW * ROWS, 256), F32)], axis=0))
        a_ref[k, :TALL, :] = high
        a_ref[k, TALL:, :] = low
        across = (((1,), (1,)), ((), ()))
        both = lax.dot_general(a_ref[k], b_ref[k, 0], across, preferred_element_type=F32)
        rest = lax.dot_general(a_ref[k, :TALL, :], b_ref[k, 1], across, preferred_element_type=F32)
        sums = (both[:TALL] + rest + both[TALL:])[: WINDOW * ROWS]
        for j in range(6):
            grid_ref[j, pl.ds(first, WINDOW)] += sums[:, 128 * j : 128 * j + 128].reshape(
                WINDOW, ROWS, 128
            )

    def two(p, carry):
        both = [(tables(2 * p + k, k), k) for k in range(2)]
        for table, k in both:
            window(span_ref[2 * (2 * p + k)], *table, k)
        for table, k in both:
            low_x, high_x = span_ref[2 * (2 * p + k)], span_ref[2 * (2 * p + k) + 1]

            def more(w, carry, table=table, k=k, low_x=low_x):
                window(low_x + WINDOW * w, *table, k)
                return carry

            lax.fori_loop(1, (high_x + 4 - low_x + WINDOW - 1) // WINDOW, more, 0)
        return carry

    lax.fori_loop(begin, end, two, 0)


def spread_edges(edges, grid_ref, patches=None):
    for edge in edges:
        edge_tile(*edge[:3], *edge[4:], grid_ref, patches)
    for edge in edges:

        def more(t, carry, edge=edge):
            edge_tile(*edge[:2], t, *edge[4:], grid_ref, patches)
            return carry

        lax.fori_loop(edge[2] + 1, edge[3], more, 0)


def edge_tile(ref, base, t, dx, dy, grid_ref, patches):
    rows = pl.ds(pl.multiple_of(base + 8 * t, 8), 8)
    (weight_x, weight_y, weight_z), forces, (base_x, base_y, base_z) = decode(
        ref[rows, :], ref[pl.ds(base + DEEP + t, 1), :]
    )
    base_x, base_y = base_x + CX * dx, base_y + CY * dy
    wz = z_table(base_z, weight_z)
    if dx == 0:
        table = x_table(ROWS, base_x, 0, weight_x)
        cells = (-1, 0, 1) if dy < 0 else (CY - 1, CY, CY + 1)
        lines = [one_row(base_y, cell, weight_y) for cell in cells]
    else:
        table = y_table(base_y, weight_y)
        cells = (-1, 0, 1) if dx < 0 else (CX - 1, CX, CX + 1)
        lines = [one_row(base_x, cell, weight_x) for cell in cells]
    a_high, a_low = split(jnp.concatenate([table * line for line in lines], axis=0))
    b_high, b_low = split(jnp.concatenate([wz * force for force in forces], axis=0))
    sums = lax.dot_general(
        jnp.concatenate([a_high, a_low, a_high], axis=1),
        jnp.concatenate([b_high, b_high, b_low], axis=1),
        (((1,), (1,)), ((), ())),
        preferred_element_type=F32,
    )
    for j in range(6):
        part = sums[:, 128 * j : 128 * j + 128]
        if dx == 0:
            for i, cell in enumerate(cells):
                row = cell % ROWS
                grid_ref[j, 0:PLANES, row, :] += part[ROWS * i : ROWS * i + PLANES]
                for (patch, at), e in zip(patches, (32, 0)):
                    at = at + patch_row(j, dy, i)
                    patch[at : at + 3, :] += part[ROWS * i + e : ROWS * i + e + 3]
        else:
            grid_ref[j, cells[0] + 1 : cells[0] + 4] += part.reshape(3, ROWS, 128)


def tiles_of(ref, base):
    return (scalar(ref[base + COUNTS : base + COUNTS + 1, :]) + 127) // 128


def patch_row(j, dy, i):
    return 24 * j + (9 if dy > 0 else 0) + 3 * i


def spread_kernel(count_ref, span_ref, list_ref, grid_ref, a_ref, b_ref, wx_ref):
    for j in range(6):
        grid_ref[j] = jnp.zeros(grid_ref.shape[1:], F32)
    spread_list(list_ref, 0, (count_ref[0] + 3) // 8, span_ref, grid_ref, a_ref, b_ref, wx_ref)


def spread(count, span, markers):
    return pl.pallas_call(
        spread_kernel,
        out_shape=jax.ShapeDtypeStruct((6, PLANES + WINDOW, ROWS, 128), F32),
        in_specs=[SMEM, SMEM, VMEM],
        out_specs=VMEM,
        compiler_params=pltpu.CompilerParams(vmem_limit_bytes=16 * MIB),
        scratch_shapes=[
            pltpu.VMEM((2, 2 * TALL, 256), BF16),
            pltpu.VMEM((2, 2, 768, 256), BF16),
            pltpu.VMEM((2, 16, 256), F32),
        ],
        cost_estimate=pl.CostEstimate(flops=6_000_000_000, bytes_accessed=6_000_000, transcendentals=0),
        name="spread",
    )(count, span, markers)


def pack_x_kernel(u_ref, rho_ref, below_ref, above_ref, list_ref, grid_in, xn_ref, xp_ref, grid_ref, sems):
    copies = []
    for c in range(4):
        for h in range(2):
            j, lanes = 2 * c + h, pl.ds(128 * h, 128)
            for n, (ref, base, x) in enumerate(
                ((xn_ref, ROWS * j, CX - 1), (xp_ref, 2 * ROWS * j, 0), (xp_ref, 2 * ROWS * j + ROWS, 1))
            ):
                src = u_ref.at[c, x, :, lanes] if c < 3 else rho_ref.at[x, :, lanes]
                copies.append(pltpu.make_async_copy(src, ref.at[pl.ds(base, CY)], sems.at[n, j]))
    for copy in copies:
        copy.start()
    for j in range(8):
        fill = jnp.full((8, 128), 0.0 if j < 6 else 1.0, F32)
        for ref, base, x in (
            (xn_ref, ROWS * j, CX - 1), (xp_ref, 2 * ROWS * j, 0), (xp_ref, 2 * ROWS * j + ROWS, 1)
        ):
            ref[base + CY : base + ROWS, :] = fill
            for r in range(2):
                row = (2 * j + r) * CX + x
                ref[base + CY + r : base + CY + r + 1, :] = above_ref[row : row + 1, :]
            ref[base + ROWS - 1 : base + ROWS, :] = below_ref[j * CX + x : j * CX + x + 1, :]
    patches = []
    for ref, base in ((xn_ref, 8 * ROWS), (xp_ref, 16 * ROWS)):
        ref[base : base + LIST, :] = list_ref[:LIST, :]
        ref[base + LIST : base + LIST + PATCH, :] = jnp.zeros((PATCH, 128), F32)
        patches.append((ref, base + LIST))
    spread_edges(
        [
            (below_ref, 8 * CX, 0, tiles_of(below_ref, 8 * CX), 0, -1),
            (above_ref, 16 * CX, 0, tiles_of(above_ref, 16 * CX), 0, 1),
        ],
        grid_ref,
        patches,
    )
    for copy in copies:
        copy.wait()


def pack_x(u_old, density, below, above, markers, grid):
    return pl.pallas_call(
        pack_x_kernel,
        out_shape=[
            jax.ShapeDtypeStruct((8 * ROWS + LIST + PATCH, 128), F32),
            jax.ShapeDtypeStruct((16 * ROWS + LIST + PATCH, 128), F32),
            jax.ShapeDtypeStruct(grid.shape, F32),
        ],
        in_specs=[HBM, HBM] + [VMEM] * 4,
        out_specs=[VMEM] * 3,
        input_output_aliases={5: 2},
        compiler_params=pltpu.CompilerParams(vmem_limit_bytes=16 * MIB),
        scratch_shapes=[pltpu.SemaphoreType.DMA((3, 8))],
        name="pack_x",
    )(u_old, density, below, above, markers, grid)


def chunk_order(span_ref, chunks, early, order_ref):
    def look(j, n):
        inside = (span_ref[2 * j] >= 3) & (span_ref[2 * j + 1] <= 28)
        order_ref[n] = j
        return n + (inside == early).astype(jnp.int32)

    n = lax.fori_loop(0, chunks, look, 0)
    order_ref[n] = TILES // 2
    return n


def interpolate(list_ref, span_ref, order_ref, n, ut_ref, a_ref, wx_ref, sorted_ref):
    wide = 128 * REACH

    def tables(j):
        (weight_x, weight_y, weight_z), _, (base_x, base_y, base_z) = chunk_of(list_ref, j)
        return weight_x, base_x, y_table(base_y, weight_y), z_table(base_z, weight_z)

    def window(g, weight_x, base_x, wy, wz, k):
        wx_ref[k] = x_table(16, base_x, 3 * g, weight_x)
        for i in range(REACH):
            three = [wx_ref[k, e : e + 1, :] * wy for e in range(3 * i, 3 * i + 3)]
            high, low = split(jnp.concatenate(three + [jnp.zeros((8, 256), F32)], axis=0))
            a_ref[k, 128 * i : 128 * i + 128, :] = high
            a_ref[k, 128 * (REACH + i) : 128 * (REACH + i) + 128, :] = low
        ut_high = ut_ref[:, pl.ds(pl.multiple_of(128 * g, 128), wide)]
        ut_low = ut_ref[:, pl.ds(pl.multiple_of(DEPTH + 128 * g, 128), wide)]
        high, low = a_ref[k, :wide, :], a_ref[k, wide:, :]
        picked = (
            jnp.dot(ut_high, high, preferred_element_type=F32)
            + jnp.dot(ut_high, low, preferred_element_type=F32)
            + jnp.dot(ut_low, high, preferred_element_type=F32)
        )
        return [jnp.sum(picked[256 * c : 256 * c + 256] * wz, axis=0, keepdims=True) for c in range(3)]

    def two(p, carry):
        chunks = [order_ref[2 * p + k] for k in range(2)]
        both = [(j, tables(j), k) for k, j in enumerate(chunks)]
        for j, table, k in both:
            lanes = pl.ds(pl.multiple_of(256 * j, 256), 256)
            first = jnp.where(j < TILES // 2, span_ref[jnp.minimum(2 * j, TILES - 2)] // 3, 0)
            for c, value in enumerate(window(first, *table, k)):
                sorted_ref[c : c + 1, lanes] = value
        for j, table, k in both:
            lanes = pl.ds(pl.multiple_of(256 * j, 256), 256)
            at = jnp.minimum(2 * j, TILES - 2)
            first, high_x = span_ref[at] // 3, jnp.where(j < TILES // 2, span_ref[at + 1], 0)

            def more(w, carry, table=table, k=k, lanes=lanes, first=first):
                for c, value in enumerate(window(first + REACH * w, *table, k)):
                    sorted_ref[c : c + 1, lanes] += value
                return carry

            lax.fori_loop(1, (high_x + 4 - 3 * first + 3 * REACH - 1) // (3 * REACH), more, 0)
        return carry

    lax.fori_loop(0, (n + 1) // 2, two, 0)


DEPTH = 128 * (GROUPS + REACH)


def advance(g, old, grid_ref, fresh_ref, ut_ref, owned):
    planes = pl.ds(3 * g, 3)
    for h in range(2):
        half_over = 0.5 / old(6 + h)
        for c in range(3):
            j = 2 * c + h
            value = old(j) + grid_ref[j, planes] * half_over
            for i, x in owned:
                fresh_ref[j, x] = value[i, :CY]
            flat = jnp.concatenate([value.reshape(3 * ROWS, 128), jnp.zeros((8, 128), F32)], axis=0)
            high, low = split(flat.T)
            rows = slice(128 * j, 128 * j + 128)
            ut_ref[rows, pl.ds(pl.multiple_of(128 * g, 128), 128)] = high
            ut_ref[rows, pl.ds(pl.multiple_of(DEPTH + 128 * g, 128), 128)] = low


def own_plane(u_ref, rho_ref, rim_ref, j, e):
    lanes = slice(128 * (j % 2), 128 * (j % 2) + 128)
    inner = u_ref[j // 2, e - 1, :, lanes] if j < 6 else rho_ref[e - 1, :, lanes]
    return jnp.concatenate([inner, rim_ref[j, e]], axis=0)


def middle_kernel(
    count_ref, span_ref, list_ref, u_ref, rho_ref, below_ref, above_ref, grid_in,
    grid_ref, fresh_ref, ut_ref, rim_ref, sorted_ref,
    spread_a, spread_b, spread_wx, a_ref, wx_ref, order_ref,
):
    count = count_ref[0]
    spread_list(
        list_ref, (count + 3) // 8, (count + 3) // 4, span_ref, grid_ref, spread_a, spread_b, spread_wx
    )
    for j in range(8):
        rim_ref[j] = jnp.full((PLANES, 8, 128), 0.0 if j < 6 else 1.0, F32)
        rim_ref[j, 1:33, 7, :] = below_ref[CX * j : CX * (j + 1), :]
        rim_ref[j, 1:33, 0, :] = above_ref[2 * CX * j : 2 * CX * j + CX, :]
        rim_ref[j, 1:33, 1, :] = above_ref[2 * CX * j + CX : 2 * CX * (j + 1), :]
    for part in range(2):
        for g, groups in ((0, 1), (11, 1 + REACH)):
            start = DEPTH * part + 128 * g
            ut_ref[:, start : start + 128 * groups] = jnp.zeros((768, 128 * groups), BF16)
    sorted_ref[...] = jnp.zeros(sorted_ref.shape, F32)

    def group(g, carry):
        def old(j):
            return jnp.stack([own_plane(u_ref, rho_ref, rim_ref, j, 3 * g + i) for i in range(3)])

        advance(g, old, grid_ref, fresh_ref, ut_ref, [(i, 3 * g + i - 1) for i in range(3)])
        return carry

    lax.fori_loop(1, 11, group, 0)
    n = chunk_order(span_ref, (count + 1) // 2, True, order_ref)
    interpolate(list_ref, span_ref, order_ref, n, ut_ref, a_ref, wx_ref, sorted_ref)


def middle(count, span, markers, u_old, density, below, above, grid):
    return pl.pallas_call(
        middle_kernel,
        out_shape=[
            jax.ShapeDtypeStruct(grid.shape, F32),
            jax.ShapeDtypeStruct((6, CX, CY, 128), F32),
            jax.ShapeDtypeStruct((768, 2 * DEPTH), BF16),
            jax.ShapeDtypeStruct((8, PLANES, 8, 128), F32),
            jax.ShapeDtypeStruct((8, 128 * TILES + 256), F32),
        ],
        in_specs=[SMEM, SMEM] + [VMEM] * 6,
        out_specs=[VMEM] * 5,
        input_output_aliases={7: 0},
        compiler_params=pltpu.CompilerParams(vmem_limit_bytes=24 * MIB),
        scratch_shapes=[
            pltpu.VMEM((2, 2 * TALL, 256), BF16),
            pltpu.VMEM((2, 2, 768, 256), BF16),
            pltpu.VMEM((2, 16, 256), F32),
            pltpu.VMEM((2, 2 * 128 * REACH, 256), BF16),
            pltpu.VMEM((2, 16, 256), F32),
            pltpu.SMEM((TILES,), jnp.int32),
        ],
        cost_estimate=pl.CostEstimate(flops=6_000_000_000, bytes_accessed=6_000_000, transcendentals=0),
        name="middle",
    )(count, span, markers, u_old, density, below, above, grid)


def finish_kernel(
    count_ref, span_ref, list_ref, pos_ref, u_ref, rho_ref, rim_ref, left_ref, right_ref,
    grid_in, fresh_in, ut_in, sorted_in,
    out_ref, vel_ref, grid_ref, fresh_ref, ut_ref, sorted_ref, a_ref, wx_ref, order_ref, out_sem,
):
    count = count_ref[0]
    lo, ro = 8 * ROWS, 16 * ROWS
    high = [scalar(left_ref[lo + COUNTS + n : lo + COUNTS + n + 1, :]) for n in (1, 2)]
    spread_edges(
        [
            (left_ref, lo, jnp.minimum(high[0] // 128, TILES - 1), (high[1] + 127) // 128, -1, 0),
            (right_ref, ro, 0, tiles_of(right_ref, ro), 1, 0),
        ],
        grid_ref,
    )
    for j in range(6):
        for ref, base, e in ((left_ref, lo + LIST, 0), (right_ref, ro + LIST, 32)):
            for dy, first in ((-1, -1), (1, CY - 1)):
                for i in range(3):
                    at = base + patch_row(j, dy, i)
                    grid_ref[j, e : e + 3, (first + i) % ROWS, :] += ref[at : at + 3, :]

    def plane(j, e):
        if e == 0:
            return left_ref[ROWS * j : ROWS * (j + 1), :]
        if e in (33, 34):
            return right_ref[ROWS * (2 * j + e - 33) : ROWS * (2 * j + e - 32), :]
        if e == 35:
            return jnp.full((ROWS, 128), 0.0 if j < 6 else 1.0, F32)
        return own_plane(u_ref, rho_ref, rim_ref, j, e)

    for g in (0, 10, 11):
        advance(
            g, lambda j, g=g: jnp.stack([plane(j, 3 * g + i) for i in range(3)]), grid_ref, fresh_ref, ut_ref,
            [(i, 3 * g + i - 1) for i in range(3) if 1 <= 3 * g + i <= CX],
        )
    outs = []
    for c in range(3):
        for h in range(2):
            outs.append(
                pltpu.make_async_copy(
                    fresh_ref.at[2 * c + h], out_ref.at[c, :, :, pl.ds(128 * h, 128)], out_sem.at[2 * c + h]
                )
            )
    for copy in outs:
        copy.start()
    n = chunk_order(span_ref, (count + 1) // 2, False, order_ref)
    interpolate(list_ref, span_ref, order_ref, n, ut_ref, a_ref, wx_ref, sorted_ref)

    parts = jnp.concatenate([p.astype(F32) for p in split3(sorted_ref[:, : 128 * TILES])], axis=0).astype(BF16)
    place = lax.broadcasted_iota(jnp.int32, (2048, 128), 0).astype(F32)
    vel_ref[...] = jnp.zeros(vel_ref.shape, F32)

    def back(p, carry):
        for t in (4 * p, 4 * p + 2):
            pick = jnp.concatenate(
                [jnp.where(place == pos_ref[pl.ds(t + h, 1), :], 1.0, 0.0).astype(BF16) for h in range(2)], axis=1
            )
            sums = jnp.dot(parts, pick, preferred_element_type=F32)
            sums = sums[0:8] + sums[8:16] + sums[16:24]
            for h in range(2):
                for c in range(3):
                    vel_ref[c, pl.ds(t + h, 1), :] = sums[c : c + 1, 128 * h : 128 * h + 128]
        return carry

    lax.fori_loop(0, (count + 3) // 4, back, 0)
    for copy in outs:
        copy.wait()


def finish(count, span, markers, pos, u_old, density, rim, left, right, grid, fresh, ut, sorted_list):
    slots = pos.shape[0]
    return pl.pallas_call(
        finish_kernel,
        out_shape=[
            jax.ShapeDtypeStruct(u_old.shape, F32),
            jax.ShapeDtypeStruct((3, slots, 128), F32),
            jax.ShapeDtypeStruct(grid.shape, F32),
            jax.ShapeDtypeStruct(fresh.shape, F32),
            jax.ShapeDtypeStruct(ut.shape, BF16),
            jax.ShapeDtypeStruct(sorted_list.shape, F32),
        ],
        in_specs=[SMEM, SMEM] + [VMEM] * 11,
        out_specs=[HBM] + [VMEM] * 5,
        input_output_aliases={9: 2, 10: 3, 11: 4, 12: 5},
        compiler_params=pltpu.CompilerParams(vmem_limit_bytes=24 * MIB),
        scratch_shapes=[
            pltpu.VMEM((2, 2 * 128 * REACH, 256), BF16),
            pltpu.VMEM((2, 16, 256), F32),
            pltpu.SMEM((TILES,), jnp.int32),
            pltpu.SemaphoreType.DMA((6,)),
        ],
        cost_estimate=pl.CostEstimate(flops=6_000_000_000, bytes_accessed=12_000_000, transcendentals=0),
        name="finish",
    )(count, span, markers, pos, u_old, density, rim, left, right, grid, fresh, ut, sorted_list)[:2]


def shift(value, axis, steps):
    count = lax.axis_size(axis)
    return lax.ppermute(value, axis, [(i, (i + steps) % count) for i in range(count)])


def on_device(u_old, density, offsets, forces, base_x, base_y, base_z, tile_count):
    arrays = (offsets, forces, base_x, base_y, base_z)
    to_next, to_previous, payload = pack_y(tile_count, arrays, u_old, density)
    below = shift(to_next, "gy", 1)
    above = shift(to_previous, "gy", -1)
    markers, pos, span = sort(tile_count, payload)
    grid = spread(tile_count, span, markers)
    to_next, to_previous, grid = pack_x(u_old, density, below, above, markers, grid)
    left = shift(to_next, "gx", 1)
    right = shift(to_previous, "gx", -1)
    grid, fresh, ut, rim, sorted_list = middle(
        tile_count, span, markers, u_old, density, below, above, grid
    )
    return finish(
        tile_count, span, markers, pos, u_old, density, rim, left, right, grid, fresh, ut, sorted_list
    )


def solution(mesh):
    in_specs = (
        P(None, "gx", "gy", None),
        P("gx", "gy", None),
        P(None, ("gx", "gy"), None),
        P(None, ("gx", "gy"), None),
        P(("gx", "gy"), None),
        P(("gx", "gy"), None),
        P(("gx", "gy"), None),
        P(("gx", "gy")),
    )
    out_specs = (P(None, "gx", "gy", None), P(None, ("gx", "gy"), None))
    return jax.shard_map(
        on_device, mesh=mesh, in_specs=in_specs, out_specs=out_specs, check_vma=False
    )
```

time: 45.3 us -> 43.7 us (0.965)
  the two profiles are of different devices: /device:TPU:13 before, /device:TPU:98 now
where the time goes in v3:
time: 43.7 us; the launch traced here: 43.6 us
  Pallas kernels  29.3 us (67%)
  starting transfers between devices  8.64 us (20%)
  waiting for transfers between devices  3.23 us (7%)
  between operations  1.53 us (4%)
  local copies, waits for them, and re-layouts  0.92 us (2%)
    pallas_call x1, Pallas kernels, middle(): pl.pallas_call(middle_kernel, out_shape=[jax.ShapeDtypeStruct(grid.shape,...  11.8 us
    ppermute x4, starting transfers between devices, shift(): lax.ppermute(value, axis, [(i, (i + steps) % count) for i in range(count)])  8.64 us
    pallas_call x1, Pallas kernels, finish(): pl.pallas_call(finish_kernel, out_shape=[jax.ShapeDtypeStruct(u_old.shape...  5.69 us
    pallas_call x1, Pallas kernels, pack_y(): pl.pallas_call(pack_y_kernel, out_shape=[jax.ShapeDtypeStruct((8 * CX + L...  3.63 us
    pallas_call x1, Pallas kernels, spread(): pl.pallas_call(spread_kernel, out_shape=jax.ShapeDtypeStruct((6, PLANES +...  3.5 us
    ppermute x4, waiting for transfers between devices, shift(): lax.ppermute(value, axis, [(i, (i + steps) % count) for i in range(count)])  3.23 us
    pallas_call x1, Pallas kernels, sort(): pl.pallas_call(sort_kernel, out_shape=[jax.ShapeDtypeStruct((LIST, 128),...  3.18 us
    pallas_call x1, Pallas kernels, pack_x(): pl.pallas_call(pack_x_kernel, out_shape=[jax.ShapeDtypeStruct((8 * ROWS +...  1.51 us
  transfers between devices with their start and end apart: 4, of which 1 were waited for; matrix products, arithmetic and copies ran while one was open for 0% of the time, Pallas kernels for 42%

profile of v3, /device:TPU:98, one launch (start us, length us, event | category | flops | bytes accessed | tf_op | source)
XLA Modules:
  0.0 43.6 jit_solution(15697388912660100090)
XLA Ops:
  1.3 3.6 %pack_y.1 = (f32[408,128]{1,0:T(8,128)}, f32[664,128]{1,0:T(8,128)}, f32[16,2048]{1,0:T(8,128)}) custom-call(s32[1]{0:T(128)S(6)} %copy.22.count_ref, f32[3,16,128]{2,1,0:T(8,128)} %off_hbm.1, f32[3,16,128]{2,1,0:T(8,128)} %force_hbm.1, s32[16,128]{1,0:T(8,128)} %bx_hbm.1, s32[16,128]{1,0:T(8,128)} %by_hbm.1, s32[16,128]{1,0:T(8,128)} %bz_hbm.1, ...), custom_call_target="tpu_custom_call" | custom-call | tf_op jit(solution)/shard_map/pack_y/pallas_call | solution.py:199
  4.9 3.2 %collective-permute-start = (f32[408,128]{1,0:T(8,128)}, f32[408,128]{1,0:T(8,128)S(1)}, u32[]{:S(2)}, u32[]{:S(2)}) collective-permute-start(f32[408,128]{1,0:T(8,128)} %get-tuple-element.22), channel_id=1, source_target_pairs={{0,1},{1,2},{2,3},{3,4},{4,5},{5,6},{6,7},{7,8},{8,9},{9,10},{10,1... | collective-permute-start | bytes 626696 | tf_op jit(solution)/shard_map/ppermute | solution.py:691
  8.1 0.0 collective-permute-start.1
  8.1 0.0 copy-start.2
  8.1 0.9 %copy-done.2 = f32[16,2048]{1,0:T(8,128)S(1)} copy-done((f32[16,2048]{1,0:T(8,128)S(1)}, f32[16,2048]{1,0:T(8,128)}, u32[]{:S(2)}) %copy-start.2) | copy-done | bytes 131096
  9.0 3.2 %sort.1 = (f32[152,128]{1,0:T(8,128)S(1)}, f32[16,128]{1,0:T(8,128)S(1)}, s32[16]{0:T(128)S(1)}) custom-call(s32[1]{0:T(128)S(6)} %copy.22.count_ref, f32[16,2048]{1,0:T(8,128)S(1)} %copy-done.2), custom_call_target="tpu_custom_call" | custom-call | flops 3000000000 | bytes 400000 | tf_op jit(solution)/shard_map/sort/pallas_call | solution.py:256
  12.2 0.0 copy-start
  12.2 0.0 copy-start.1
  12.2 3.5 %spread.1.grid_in = f32[6,45,40,128]{3,2,1,0:T(8,128)S(1)} custom-call(s32[1]{0:T(128)S(6)} %copy.22.count_ref, s32[16]{0:T(128)S(1)} %get-tuple-element.19.span_ref, f32[152,128]{1,0:T(8,128)S(1)} %get-tuple-element.20.list_ref), custom_call_target="tpu_custom_call" | custom-call | flops 6000000000 | bytes 6000000 | tf_op jit(solution)/shard_map/spread/pallas_call | solution.py:377
  15.7 0.0 collective-permute-done.below_ref
  15.8 3.2 %collective-permute-done.1.above_ref = f32[664,128]{1,0:T(8,128)S(1)} collective-permute-done((f32[664,128]{1,0:T(8,128)}, f32[664,128]{1,0:T(8,128)S(1)}, u32[]{:S(2)}, u32[]{:S(2)}) %collective-permute-start.1) | collective-permute-done | bytes 340000 | tf_op jit(solution)/shard_map/ppermute | solution.py:691
  19.0 0.0 copy-done
  19.0 0.0 copy-done.1
  19.0 1.5 %pack_x.1 = (f32[616,128]{1,0:T(8,128)S(1)}, f32[936,128]{1,0:T(8,128)S(1)}, f32[6,45,40,128]{3,2,1,0:T(8,128)S(1)}) custom-call(f32[3,32,32,256]{3,2,1,0:T(8,128)S(1)} %copy-done, f32[32,32,256]{2,1,0:T(8,128)S(1)} %copy-done.1, f32[408,128]{1,0:T(8,128)S(1)} %collective-permute-done.below_ref, ...), custom_call_target="tpu_custom_call", output_to_operand_aliasing={{2}: (5, {})} | custom-call | tf_op jit(solution)/shard_map/pack_x/pallas_call | solution.py:433
  20.5 0.1 collective-permute-start.2
  20.6 5.3 %collective-permute-start.3 = (f32[936,128]{1,0:T(8,128)S(1)}, f32[936,128]{1,0:T(8,128)S(1)}, u32[]{:S(2)}, u32[]{:S(2)}) collective-permute-start(f32[936,128]{1,0:T(8,128)S(1)} %get-tuple-element.27), channel_id=1, source_target_pairs={{0,240},{16,0},{32,16},{48,32},{64,48},{80,64},{96,80},{112,96},{1... | collective-permute-start | bytes 1437704 | tf_op jit(solution)/shard_map/ppermute | solution.py:691
  25.9 11.8 %middle.1 = (f32[6,45,40,128]{3,2,1,0:T(8,128)S(1)}, f32[6,32,32,128]{3,2,1,0:T(8,128)S(1)}, bf16[768,4096]{1,0:T(8,128)(2,1)S(1)}, f32[8,36,8,128]{3,2,1,0:T(8,128)S(1)}, f32[8,2304]{1,0:T(8,128)S(1)}) custom-call(s32[1]{0:T(128)S(6)} %copy.22.count_ref, s32[16]{0:T(128)S(1)} %get-tuple-element.19.span_ref, ...), custom_call_target="tpu_custom_call", output_to_operand_aliasing={{0}: (7, {})} | custom-call | flops 6000000000 | bytes 6000000 | tf_op jit(solution)/shard_map/middle/pallas_call | solution.py:566
  37.7 0.0 collective-permute-done.2.left_ref
  37.7 0.0 collective-permute-done.3.right_ref
  37.7 5.7 %finish.1 = (f32[3,32,32,256]{3,2,1,0:T(8,128)}, f32[3,16,128]{2,1,0:T(8,128)}, f32[6,45,40,128]{3,2,1,0:T(8,128)S(1)}, f32[6,32,32,128]{3,2,1,0:T(8,128)S(1)}, ...) custom-call(s32[1]{0:T(128)S(6)} %copy.22.count_ref, ...), custom_call_target="tpu_custom_call", output_to_operand_aliasing={{2}: (9, {}), {3}: (10, {}), {4}: (11, {}), {5}: (12, {})} | custom-call | flops 6000000000 | bytes 12000000 | tf_op jit(solution)/shard_map/finish/pallas_call | solution.py:664
Async XLA Ops:
  4.9 10.8 %collective-permute-start = (f32[408,128]{1,0:T(8,128)}, f32[408,128]{1,0:T(8,128)S(1)}, u32[]{:S(2)}, u32[]{:S(2)}) collective-permute-start(f32[408,128]{1,0:T(8,128)} %get-tuple-element.22), channel_id=1, source_target_pairs={{0,1},{1,2},{2,3},{3,4},{4,5},{5,6},{6,7},{7,8},{8,9},{9,10},{10,1... | collective-permute-start | bytes 626696 | tf_op jit(solution)/shard_map/ppermute | solution.py:691
  8.1 10.9 %collective-permute-start.1 = (f32[664,128]{1,0:T(8,128)}, f32[664,128]{1,0:T(8,128)S(1)}, u32[]{:S(2)}, u32[]{:S(2)}) collective-permute-start(f32[664,128]{1,0:T(8,128)} %get-tuple-element.23), channel_id=1, source_target_pairs={{0,15},{1,0},{2,1},{3,2},{4,3},{5,4},{6,5},{7,6},{8,7},{9,8},{10,9... | collective-permute-start | bytes 1019912 | tf_op jit(solution)/shard_map/ppermute | solution.py:691
  8.1 0.9 %copy-start.2 = (f32[16,2048]{1,0:T(8,128)S(1)}, f32[16,2048]{1,0:T(8,128)}, u32[]{:S(2)}) copy-start(f32[16,2048]{1,0:T(8,128)} %get-tuple-element.18.pay_ref) | copy-start | bytes 393220
  12.2 6.8 %copy-start = (f32[3,32,32,256]{3,2,1,0:T(8,128)S(1)}, f32[3,32,32,256]{3,2,1,0:T(8,128)}, u32[]{:S(2)}) copy-start(f32[3,32,32,256]{3,2,1,0:T(8,128)} %u_ref.7) | copy-start | bytes 9437188
  12.2 6.8 %copy-start.1 = (f32[32,32,256]{2,1,0:T(8,128)S(1)}, f32[32,32,256]{2,1,0:T(8,128)}, u32[]{:S(2)}) copy-start(f32[32,32,256]{2,1,0:T(8,128)} %rho_ref.7) | copy-start | bytes 3145732
  20.5 17.2 %collective-permute-start.2 = (f32[616,128]{1,0:T(8,128)S(1)}, f32[616,128]{1,0:T(8,128)S(1)}, u32[]{:S(2)}, u32[]{:S(2)}) collective-permute-start(f32[616,128]{1,0:T(8,128)S(1)} %get-tuple-element.26), channel_id=1, source_target_pairs={{0,16},{16,32},{32,48},{48,64},{64,80},{80,96},{96,112},{112,128},... | collective-permute-start | bytes 946184 | tf_op jit(solution)/shard_map/ppermute | solution.py:691
  20.6 17.1 %collective-permute-start.3 = (f32[936,128]{1,0:T(8,128)S(1)}, f32[936,128]{1,0:T(8,128)S(1)}, u32[]{:S(2)}, u32[]{:S(2)}) collective-permute-start(f32[936,128]{1,0:T(8,128)S(1)} %get-tuple-element.27), channel_id=1, source_target_pairs={{0,240},{16,0},{32,16},{48,32},{64,48},{80,64},{96,80},{112,96},{1... | collective-permute-start | bytes 1437704 | tf_op jit(solution)/shard_map/ppermute | solution.py:691

commit v4 on v3

--- a/solution.py
+++ b/solution.py
@@ -269,7 +269,7 @@
     )(count, payload)
 
 
-def spread_list(list_ref, begin, end, span_ref, grid_ref, a_ref, b_ref, wx_ref):
+def spread_list(list_ref, pairs, span_ref, grid_ref, a_ref, b_ref, wx_ref):
     def tables(j, k):
         (weight_x, weight_y, weight_z), forces, (base_x, base_y, base_z) = chunk_of(list_ref, j)
         wy, wz = y_table(base_y, weight_y), z_table(base_z, weight_z)
@@ -308,7 +308,7 @@
             lax.fori_loop(1, (high_x + 4 - low_x + WINDOW - 1) // WINDOW, more, 0)
         return carry
 
-    lax.fori_loop(begin, end, two, 0)
+    lax.fori_loop(0, pairs, two, 0)
 
 
 def spread_edges(edges, grid_ref, patches=None):
@@ -370,7 +370,7 @@
 def spread_kernel(count_ref, span_ref, list_ref, grid_ref, a_ref, b_ref, wx_ref):
     for j in range(6):
         grid_ref[j] = jnp.zeros(grid_ref.shape[1:], F32)
-    spread_list(list_ref, 0, (count_ref[0] + 3) // 8, span_ref, grid_ref, a_ref, b_ref, wx_ref)
+    spread_list(list_ref, (count_ref[0] + 3) // 4, span_ref, grid_ref, a_ref, b_ref, wx_ref)
 
 
 def spread(count, span, markers):
@@ -446,11 +446,13 @@
     )(u_old, density, below, above, markers, grid)
 
 
-def chunk_order(span_ref, chunks, early, order_ref):
+OUTER = (0, 10, 11)
+
+
+def outer_chunks(span_ref, chunks, order_ref):
     def look(j, n):
-        inside = (span_ref[2 * j] >= 3) & (span_ref[2 * j + 1] <= 28)
         order_ref[n] = j
-        return n + (inside == early).astype(jnp.int32)
+        return n + ((span_ref[2 * j] < 3) | (span_ref[2 * j + 1] > 28)).astype(jnp.int32)
 
     n = lax.fori_loop(0, chunks, look, 0)
     order_ref[n] = TILES // 2
@@ -458,21 +460,27 @@
 
 
 def interpolate(list_ref, span_ref, order_ref, n, ut_ref, a_ref, wx_ref, sorted_ref):
-    wide = 128 * REACH
+    outer = order_ref is not None
+    reach = len(OUTER) if outer else REACH
+    wide = 128 * reach
 
     def tables(j):
         (weight_x, weight_y, weight_z), _, (base_x, base_y, base_z) = chunk_of(list_ref, j)
         return weight_x, base_x, y_table(base_y, weight_y), z_table(base_z, weight_z)
 
     def window(g, weight_x, base_x, wy, wz, k):
-        wx_ref[k] = x_table(16, base_x, 3 * g, weight_x)
-        for i in range(REACH):
-            three = [wx_ref[k, e : e + 1, :] * wy for e in range(3 * i, 3 * i + 3)]
+        wx_ref[k] = x_table(wx_ref.shape[1], base_x, 3 * g, weight_x)
+        for i in range(reach):
+            at = 3 * (OUTER[i] if outer else i)
+            three = [wx_ref[k, e : e + 1, :] * wy for e in range(at, at + 3)]
             high, low = split(jnp.concatenate(three + [jnp.zeros((8, 256), F32)], axis=0))
             a_ref[k, 128 * i : 128 * i + 128, :] = high
-            a_ref[k, 128 * (REACH + i) : 128 * (REACH + i) + 128, :] = low
-        ut_high = ut_ref[:, pl.ds(pl.multiple_of(128 * g, 128), wide)]
-        ut_low = ut_ref[:, pl.ds(pl.multiple_of(DEPTH + 128 * g, 128), wide)]
+            a_ref[k, wide + 128 * i : wide + 128 * i + 128, :] = low
+        if outer:
+            ut_high, ut_low = ut_ref[:, :wide], ut_ref[:, wide:]
+        else:
+            ut_high = ut_ref[:, pl.ds(pl.multiple_of(128 * g, 128), wide)]
+            ut_low = ut_ref[:, pl.ds(pl.multiple_of(DEPTH + 128 * g, 128), wide)]
         high, low = a_ref[k, :wide, :], a_ref[k, wide:, :]
         picked = (
             jnp.dot(ut_high, high, preferred_element_type=F32)
@@ -482,17 +490,18 @@
         return [jnp.sum(picked[256 * c : 256 * c + 256] * wz, axis=0, keepdims=True) for c in range(3)]
 
     def two(p, carry):
-        chunks = [order_ref[2 * p + k] for k in range(2)]
+        chunks = [order_ref[2 * p + k] if outer else 2 * p + k for k in range(2)]
         both = [(j, tables(j), k) for k, j in enumerate(chunks)]
         for j, table, k in both:
             lanes = pl.ds(pl.multiple_of(256 * j, 256), 256)
-            first = jnp.where(j < TILES // 2, span_ref[jnp.minimum(2 * j, TILES - 2)] // 3, 0)
+            first = 0 if outer else span_ref[2 * j] // 3
             for c, value in enumerate(window(first, *table, k)):
-                sorted_ref[c : c + 1, lanes] = value
+                sorted_ref[c : c + 1, lanes] += value
+        if outer:
+            return carry
         for j, table, k in both:
             lanes = pl.ds(pl.multiple_of(256 * j, 256), 256)
-            at = jnp.minimum(2 * j, TILES - 2)
-            first, high_x = span_ref[at] // 3, jnp.where(j < TILES // 2, span_ref[at + 1], 0)
+            first, high_x = span_ref[2 * j] // 3, span_ref[2 * j + 1]
 
             def more(w, carry, table=table, k=k, lanes=lanes, first=first):
                 for c, value in enumerate(window(first + REACH * w, *table, k)):
@@ -508,8 +517,7 @@
 DEPTH = 128 * (GROUPS + REACH)
 
 
-def advance(g, old, grid_ref, fresh_ref, ut_ref, owned):
-    planes = pl.ds(3 * g, 3)
+def advance(planes, old, grid_ref, fresh_ref, owned, ut_ref, at, depth, known=(True, True, True)):
     for h in range(2):
         half_over = 0.5 / old(6 + h)
         for c in range(3):
@@ -517,11 +525,11 @@
             value = old(j) + grid_ref[j, planes] * half_over
             for i, x in owned:
                 fresh_ref[j, x] = value[i, :CY]
-            flat = jnp.concatenate([value.reshape(3 * ROWS, 128), jnp.zeros((8, 128), F32)], axis=0)
-            high, low = split(flat.T)
+            kept = [value[i] if known[i] else jnp.zeros((ROWS, 128), F32) for i in range(3)]
+            high, low = split(jnp.concatenate(kept + [jnp.zeros((8, 128), F32)], axis=0).T)
             rows = slice(128 * j, 128 * j + 128)
-            ut_ref[rows, pl.ds(pl.multiple_of(128 * g, 128), 128)] = high
-            ut_ref[rows, pl.ds(pl.multiple_of(DEPTH + 128 * g, 128), 128)] = low
+            ut_ref[rows, pl.ds(at, 128)] = high
+            ut_ref[rows, pl.ds(depth + at, 128)] = low
 
 
 def own_plane(u_ref, rho_ref, rim_ref, j, e):
@@ -531,14 +539,10 @@
 
 
 def middle_kernel(
-    count_ref, span_ref, list_ref, u_ref, rho_ref, below_ref, above_ref, grid_in,
-    grid_ref, fresh_ref, ut_ref, rim_ref, sorted_ref,
-    spread_a, spread_b, spread_wx, a_ref, wx_ref, order_ref,
+    count_ref, span_ref, list_ref, u_ref, rho_ref, below_ref, above_ref, grid_ref,
+    fresh_ref, rim_ref, sorted_ref, ut_ref, a_ref, wx_ref,
 ):
     count = count_ref[0]
-    spread_list(
-        list_ref, (count + 3) // 8, (count + 3) // 4, span_ref, grid_ref, spread_a, spread_b, spread_wx
-    )
     for j in range(8):
         rim_ref[j] = jnp.full((PLANES, 8, 128), 0.0 if j < 6 else 1.0, F32)
         rim_ref[j, 1:33, 7, :] = below_ref[CX * j : CX * (j + 1), :]
@@ -550,39 +554,38 @@
             ut_ref[:, start : start + 128 * groups] = jnp.zeros((768, 128 * groups), BF16)
     sorted_ref[...] = jnp.zeros(sorted_ref.shape, F32)
 
+    def old(g):
+        return lambda j: jnp.stack([own_plane(u_ref, rho_ref, rim_ref, j, 3 * g + i) for i in range(3)])
+
     def group(g, carry):
-        def old(j):
-            return jnp.stack([own_plane(u_ref, rho_ref, rim_ref, j, 3 * g + i) for i in range(3)])
-
-        advance(g, old, grid_ref, fresh_ref, ut_ref, [(i, 3 * g + i - 1) for i in range(3)])
+        advance(
+            pl.ds(3 * g, 3), old(g), grid_ref, fresh_ref, [(i, 3 * g + i - 1) for i in range(3)],
+            ut_ref, pl.multiple_of(128 * g, 128), DEPTH,
+        )
         return carry
 
-    lax.fori_loop(1, 11, group, 0)
-    n = chunk_order(span_ref, (count + 1) // 2, True, order_ref)
-    interpolate(list_ref, span_ref, order_ref, n, ut_ref, a_ref, wx_ref, sorted_ref)
+    lax.fori_loop(1, 10, group, 0)
+    advance(
+        pl.ds(30, 3), old(10), grid_ref, fresh_ref, [(0, 29), (1, 30)], ut_ref, 1280, DEPTH, (True, True, False)
+    )
+    interpolate(list_ref, span_ref, None, 2 * ((count + 3) // 4), ut_ref, a_ref, wx_ref, sorted_ref)
 
 
 def middle(count, span, markers, u_old, density, below, above, grid):
     return pl.pallas_call(
         middle_kernel,
         out_shape=[
-            jax.ShapeDtypeStruct(grid.shape, F32),
             jax.ShapeDtypeStruct((6, CX, CY, 128), F32),
-            jax.ShapeDtypeStruct((768, 2 * DEPTH), BF16),
             jax.ShapeDtypeStruct((8, PLANES, 8, 128), F32),
             jax.ShapeDtypeStruct((8, 128 * TILES + 256), F32),
         ],
         in_specs=[SMEM, SMEM] + [VMEM] * 6,
-        out_specs=[VMEM] * 5,
-        input_output_aliases={7: 0},
+        out_specs=[VMEM] * 3,
         compiler_params=pltpu.CompilerParams(vmem_limit_bytes=24 * MIB),
         scratch_shapes=[
-            pltpu.VMEM((2, 2 * TALL, 256), BF16),
-            pltpu.VMEM((2, 2, 768, 256), BF16),
-            pltpu.VMEM((2, 16, 256), F32),
+            pltpu.VMEM((768, 2 * DEPTH), BF16),
             pltpu.VMEM((2, 2 * 128 * REACH, 256), BF16),
             pltpu.VMEM((2, 16, 256), F32),
-            pltpu.SMEM((TILES,), jnp.int32),
         ],
         cost_estimate=pl.CostEstimate(flops=6_000_000_000, bytes_accessed=6_000_000, transcendentals=0),
         name="middle",
@@ -591,8 +594,8 @@
 
 def finish_kernel(
     count_ref, span_ref, list_ref, pos_ref, u_ref, rho_ref, rim_ref, left_ref, right_ref,
-    grid_in, fresh_in, ut_in, sorted_in,
-    out_ref, vel_ref, grid_ref, fresh_ref, ut_ref, sorted_ref, a_ref, wx_ref, order_ref, out_sem,
+    grid_in, fresh_in, sorted_in,
+    out_ref, vel_ref, grid_ref, fresh_ref, sorted_ref, ut_ref, a_ref, wx_ref, order_ref, out_sem,
 ):
     count = count_ref[0]
     lo, ro = 8 * ROWS, 16 * ROWS
@@ -620,10 +623,12 @@
             return jnp.full((ROWS, 128), 0.0 if j < 6 else 1.0, F32)
         return own_plane(u_ref, rho_ref, rim_ref, j, e)
 
-    for g in (0, 10, 11):
+    for n, g in enumerate(OUTER):
+        known = [e < 3 or e > CX - 1 for e in range(3 * g, 3 * g + 3)]
         advance(
-            g, lambda j, g=g: jnp.stack([plane(j, 3 * g + i) for i in range(3)]), grid_ref, fresh_ref, ut_ref,
-            [(i, 3 * g + i - 1) for i in range(3) if 1 <= 3 * g + i <= CX],
+            pl.ds(3 * g, 3), lambda j, g=g: jnp.stack([plane(j, 3 * g + i) for i in range(3)]), grid_ref, fresh_ref,
+            [(i, 3 * g + i - 1) for i in range(3) if known[i] and 1 <= 3 * g + i <= CX],
+            ut_ref, 128 * n, 128 * len(OUTER), known,
         )
     outs = []
     for c in range(3):
@@ -635,7 +640,7 @@
             )
     for copy in outs:
         copy.start()
-    n = chunk_order(span_ref, (count + 1) // 2, False, order_ref)
+    n = outer_chunks(span_ref, (count + 1) // 2, order_ref)
     interpolate(list_ref, span_ref, order_ref, n, ut_ref, a_ref, wx_ref, sorted_ref)
 
     parts = jnp.concatenate([p.astype(F32) for p in split3(sorted_ref[:, : 128 * TILES])], axis=0).astype(BF16)
@@ -659,7 +664,7 @@
         copy.wait()
 
 
-def finish(count, span, markers, pos, u_old, density, rim, left, right, grid, fresh, ut, sorted_list):
+def finish(count, span, markers, pos, u_old, density, rim, left, right, grid, fresh, sorted_list):
     slots = pos.shape[0]
     return pl.pallas_call(
         finish_kernel,
@@ -668,22 +673,22 @@
             jax.ShapeDtypeStruct((3, slots, 128), F32),
             jax.ShapeDtypeStruct(grid.shape, F32),
             jax.ShapeDtypeStruct(fresh.shape, F32),
-            jax.ShapeDtypeStruct(ut.shape, BF16),
             jax.ShapeDtypeStruct(sorted_list.shape, F32),
         ],
-        in_specs=[SMEM, SMEM] + [VMEM] * 11,
-        out_specs=[HBM] + [VMEM] * 5,
-        input_output_aliases={9: 2, 10: 3, 11: 4, 12: 5},
+        in_specs=[SMEM, SMEM] + [VMEM] * 10,
+        out_specs=[HBM] + [VMEM] * 4,
+        input_output_aliases={9: 2, 10: 3, 11: 4},
         compiler_params=pltpu.CompilerParams(vmem_limit_bytes=24 * MIB),
         scratch_shapes=[
-            pltpu.VMEM((2, 2 * 128 * REACH, 256), BF16),
-            pltpu.VMEM((2, 16, 256), F32),
+            pltpu.VMEM((768, 2 * 128 * len(OUTER)), BF16),
+            pltpu.VMEM((2, 2 * 128 * len(OUTER), 256), BF16),
+            pltpu.VMEM((2, ROWS, 256), F32),
             pltpu.SMEM((TILES,), jnp.int32),
             pltpu.SemaphoreType.DMA((6,)),
         ],
         cost_estimate=pl.CostEstimate(flops=6_000_000_000, bytes_accessed=12_000_000, transcendentals=0),
         name="finish",
-    )(count, span, markers, pos, u_old, density, rim, left, right, grid, fresh, ut, sorted_list)[:2]
+    )(count, span, markers, pos, u_old, density, rim, left, right, grid, fresh, sorted_list)[:2]
 
 
 def shift(value, axis, steps):
@@ -701,11 +706,11 @@
     to_next, to_previous, grid = pack_x(u_old, density, below, above, markers, grid)
     left = shift(to_next, "gx", 1)
     right = shift(to_previous, "gx", -1)
-    grid, fresh, ut, rim, sorted_list = middle(
+    fresh, rim, sorted_list = middle(
         tile_count, span, markers, u_old, density, below, above, grid
     )
     return finish(
-        tile_count, span, markers, pos, u_old, density, rim, left, right, grid, fresh, ut, sorted_list
+        tile_count, span, markers, pos, u_old, density, rim, left, right, grid, fresh, sorted_list
     )
 
 

time: 43.7 us -> 42.2 us (0.966)
  the two profiles are of different devices: /device:TPU:98 before, /device:TPU:13 now
where the time goes in v4:
time: 42.2 us; the launch traced here: 42 us
  Pallas kernels  27.8 us (66%)
  starting transfers between devices  11.8 us (28%)
  between operations  1.55 us (4%)
  local copies, waits for them, and re-layouts  0.92 us (2%)
    ppermute x4, starting transfers between devices, shift(): lax.ppermute(value, axis, [(i, (i + steps) % count) for i in range(count)])  11.8 us
    pallas_call x1, Pallas kernels, middle(): pl.pallas_call(middle_kernel, out_shape=[jax.ShapeDtypeStruct((6, CX, CY,...  9.47 us
    pallas_call x1, Pallas kernels, spread(): pl.pallas_call(spread_kernel, out_shape=jax.ShapeDtypeStruct((6, PLANES +...  5.49 us
    pallas_call x1, Pallas kernels, finish(): pl.pallas_call(finish_kernel, out_shape=[jax.ShapeDtypeStruct(u_old.shape...  5.08 us
    pallas_call x1, Pallas kernels, pack_y(): pl.pallas_call(pack_y_kernel, out_shape=[jax.ShapeDtypeStruct((8 * CX + L...  3.63 us
    pallas_call x1, Pallas kernels, sort(): pl.pallas_call(sort_kernel, out_shape=[jax.ShapeDtypeStruct((LIST, 128),...  2.59 us
    pallas_call x1, Pallas kernels, pack_x(): pl.pallas_call(pack_x_kernel, out_shape=[jax.ShapeDtypeStruct((8 * ROWS +...  1.52 us
    unnamed x6, local copies, waits for them, and re-layouts  0.92 us
  transfers between devices with their start and end apart: 4, of which 0 were waited for; matrix products, arithmetic and copies ran while one was open for 0% of the time, Pallas kernels for 42%

profile of v4, /device:TPU:13, one launch (start us, length us, event | category | flops | bytes accessed | tf_op | source)
XLA Modules:
  0.0 42.0 jit_solution(14220754997740956211)
XLA Ops:
  1.3 3.6 %pack_y.1 = (f32[408,128]{1,0:T(8,128)}, f32[664,128]{1,0:T(8,128)}, f32[16,2048]{1,0:T(8,128)}) custom-call(s32[1]{0:T(128)S(6)} %copy.18.count_ref, f32[3,16,128]{2,1,0:T(8,128)} %off_hbm.1, f32[3,16,128]{2,1,0:T(8,128)} %force_hbm.1, s32[16,128]{1,0:T(8,128)} %bx_hbm.1, s32[16,128]{1,0:T(8,128)} %by_hbm.1, s32[16,128]{1,0:T(8,128)} %bz_hbm.1, ...), custom_call_target="tpu_custom_call" | custom-call | tf_op jit(solution)/shard_map/pack_y/pallas_call | solution.py:199
  4.9 1.7 %collective-permute-start = (f32[408,128]{1,0:T(8,128)}, f32[408,128]{1,0:T(8,128)S(1)}, u32[]{:S(2)}, u32[]{:S(2)}) collective-permute-start(f32[408,128]{1,0:T(8,128)} %get-tuple-element.20), channel_id=1, source_target_pairs={{0,1},{1,2},{2,3},{3,4},{4,5},{5,6},{6,7},{7,8},{8,9},{9,10},{10,1... | collective-permute-start | bytes 626696 | tf_op jit(solution)/shard_map/ppermute | solution.py:696
  6.6 4.7 %collective-permute-start.1 = (f32[664,128]{1,0:T(8,128)}, f32[664,128]{1,0:T(8,128)S(1)}, u32[]{:S(2)}, u32[]{:S(2)}) collective-permute-start(f32[664,128]{1,0:T(8,128)} %get-tuple-element.21), channel_id=1, source_target_pairs={{0,15},{1,0},{2,1},{3,2},{4,3},{5,4},{6,5},{7,6},{8,7},{9,8},{10,9... | collective-permute-start | bytes 1019912 | tf_op jit(solution)/shard_map/ppermute | solution.py:696
  11.3 0.0 copy-start.2
  11.3 0.9 %copy-done.2 = f32[16,2048]{1,0:T(8,128)S(1)} copy-done((f32[16,2048]{1,0:T(8,128)S(1)}, f32[16,2048]{1,0:T(8,128)}, u32[]{:S(2)}) %copy-start.2) | copy-done | bytes 131096
  12.2 2.6 %sort.1 = (f32[152,128]{1,0:T(8,128)S(1)}, f32[16,128]{1,0:T(8,128)S(1)}, s32[16]{0:T(128)S(1)}) custom-call(s32[1]{0:T(128)S(6)} %copy.18.count_ref, f32[16,2048]{1,0:T(8,128)S(1)} %copy-done.2), custom_call_target="tpu_custom_call" | custom-call | flops 3000000000 | bytes 400000 | tf_op jit(solution)/shard_map/sort/pallas_call | solution.py:256
  14.8 0.0 copy-start
  14.8 0.0 copy-start.1
  14.8 5.5 %spread.1.grid_in = f32[6,45,40,128]{3,2,1,0:T(8,128)S(1)} custom-call(s32[1]{0:T(128)S(6)} %copy.18.count_ref, s32[16]{0:T(128)S(1)} %get-tuple-element.17.span_ref, f32[152,128]{1,0:T(8,128)S(1)} %get-tuple-element.18.list_ref), custom_call_target="tpu_custom_call" | custom-call | flops 6000000000 | bytes 6000000 | tf_op jit(solution)/shard_map/spread/pallas_call | solution.py:377
  20.3 0.0 collective-permute-done.below_ref
  20.3 0.0 collective-permute-done.1.above_ref
  20.3 0.0 copy-done
  20.3 0.0 copy-done.1
  20.4 1.5 %pack_x.1 = (f32[616,128]{1,0:T(8,128)S(1)}, f32[936,128]{1,0:T(8,128)S(1)}, f32[6,45,40,128]{3,2,1,0:T(8,128)S(1)}) custom-call(f32[3,32,32,256]{3,2,1,0:T(8,128)S(1)} %copy-done, f32[32,32,256]{2,1,0:T(8,128)S(1)} %copy-done.1, f32[408,128]{1,0:T(8,128)S(1)} %collective-permute-done.below_ref, ...), custom_call_target="tpu_custom_call", output_to_operand_aliasing={{2}: (5, {})} | custom-call | tf_op jit(solution)/shard_map/pack_x/pallas_call | solution.py:433
  21.9 5.4 %collective-permute-start.2 = (f32[616,128]{1,0:T(8,128)S(1)}, f32[616,128]{1,0:T(8,128)S(1)}, u32[]{:S(2)}, u32[]{:S(2)}) collective-permute-start(f32[616,128]{1,0:T(8,128)S(1)} %get-tuple-element.24), channel_id=1, source_target_pairs={{0,16},{16,32},{32,48},{48,64},{64,80},{80,96},{96,112},{112,128},... | collective-permute-start | bytes 946184 | tf_op jit(solution)/shard_map/ppermute | solution.py:696
  27.3 0.0 collective-permute-start.3
  27.3 9.5 %middle.1 = (f32[6,32,32,128]{3,2,1,0:T(8,128)S(1)}, f32[8,36,8,128]{3,2,1,0:T(8,128)S(1)}, f32[8,2304]{1,0:T(8,128)S(1)}) custom-call(s32[1]{0:T(128)S(6)} %copy.18.count_ref, s32[16]{0:T(128)S(1)} %get-tuple-element.17.span_ref, f32[152,128]{1,0:T(8,128)S(1)} %get-tuple-element.18.list_ref, f32[3,32,32,256]{3,2,1,0:T(8,128)S(1)} %copy-done, ...), custom_call_target="tpu_custom_call" | custom-call | flops 6000000000 | bytes 6000000 | tf_op jit(solution)/shard_map/middle/pallas_call | solution.py:575
  36.8 0.0 collective-permute-done.2.left_ref
  36.8 0.0 collective-permute-done.3.right_ref
  36.8 5.1 %finish.1 = (f32[3,32,32,256]{3,2,1,0:T(8,128)}, f32[3,16,128]{2,1,0:T(8,128)}, f32[6,45,40,128]{3,2,1,0:T(8,128)S(1)}, f32[6,32,32,128]{3,2,1,0:T(8,128)S(1)}, f32[8,2304]{1,0:T(8,128)S(1)}) custom-call(s32[1]{0:T(128)S(6)} %copy.18.count_ref, s32[16]{0:T(128)S(1)} %get-tuple-element.17.span_ref, ...), custom_call_target="tpu_custom_call", output_to_operand_aliasing={{2}: (9, {}), {3}: (10, {}), {4}: (11, {})} | custom-call | flops 6000000000 | bytes 12000000 | tf_op jit(solution)/shard_map/finish/pallas_call | solution.py:669
Async XLA Ops:
  4.9 15.4 %collective-permute-start = (f32[408,128]{1,0:T(8,128)}, f32[408,128]{1,0:T(8,128)S(1)}, u32[]{:S(2)}, u32[]{:S(2)}) collective-permute-start(f32[408,128]{1,0:T(8,128)} %get-tuple-element.20), channel_id=1, source_target_pairs={{0,1},{1,2},{2,3},{3,4},{4,5},{5,6},{6,7},{7,8},{8,9},{9,10},{10,1... | collective-permute-start | bytes 626696 | tf_op jit(solution)/shard_map/ppermute | solution.py:696
  6.6 13.7 %collective-permute-start.1 = (f32[664,128]{1,0:T(8,128)}, f32[664,128]{1,0:T(8,128)S(1)}, u32[]{:S(2)}, u32[]{:S(2)}) collective-permute-start(f32[664,128]{1,0:T(8,128)} %get-tuple-element.21), channel_id=1, source_target_pairs={{0,15},{1,0},{2,1},{3,2},{4,3},{5,4},{6,5},{7,6},{8,7},{9,8},{10,9... | collective-permute-start | bytes 1019912 | tf_op jit(solution)/shard_map/ppermute | solution.py:696
  11.3 0.9 %copy-start.2 = (f32[16,2048]{1,0:T(8,128)S(1)}, f32[16,2048]{1,0:T(8,128)}, u32[]{:S(2)}) copy-start(f32[16,2048]{1,0:T(8,128)} %get-tuple-element.16.pay_ref) | copy-start | bytes 393220
  14.8 5.5 %copy-start = (f32[3,32,32,256]{3,2,1,0:T(8,128)S(1)}, f32[3,32,32,256]{3,2,1,0:T(8,128)}, u32[]{:S(2)}) copy-start(f32[3,32,32,256]{3,2,1,0:T(8,128)} %u_ref.7) | copy-start | bytes 9437188
  14.8 5.5 %copy-start.1 = (f32[32,32,256]{2,1,0:T(8,128)S(1)}, f32[32,32,256]{2,1,0:T(8,128)}, u32[]{:S(2)}) copy-start(f32[32,32,256]{2,1,0:T(8,128)} %rho_ref.7) | copy-start | bytes 3145732
  21.9 14.9 %collective-permute-start.2 = (f32[616,128]{1,0:T(8,128)S(1)}, f32[616,128]{1,0:T(8,128)S(1)}, u32[]{:S(2)}, u32[]{:S(2)}) collective-permute-start(f32[616,128]{1,0:T(8,128)S(1)} %get-tuple-element.24), channel_id=1, source_target_pairs={{0,16},{16,32},{32,48},{48,64},{64,80},{80,96},{96,112},{112,128},... | collective-permute-start | bytes 946184 | tf_op jit(solution)/shard_map/ppermute | solution.py:696
  27.3 9.5 %collective-permute-start.3 = (f32[936,128]{1,0:T(8,128)S(1)}, f32[936,128]{1,0:T(8,128)S(1)}, u32[]{:S(2)}, u32[]{:S(2)}) collective-permute-start(f32[936,128]{1,0:T(8,128)S(1)} %get-tuple-element.25), channel_id=1, source_target_pairs={{0,240},{16,0},{32,16},{48,32},{64,48},{80,64},{96,80},{112,96},{1... | collective-permute-start | bytes 1437704 | tf_op jit(solution)/shard_map/ppermute | solution.py:696

commit v5 on v4

--- a/solution.py
+++ b/solution.py
@@ -539,10 +539,8 @@
 
 
 def middle_kernel(
-    count_ref, span_ref, list_ref, u_ref, rho_ref, below_ref, above_ref, grid_ref,
-    fresh_ref, rim_ref, sorted_ref, ut_ref, a_ref, wx_ref,
+    u_ref, rho_ref, below_ref, above_ref, grid_ref, fresh_ref, rim_ref, ut_ref,
 ):
-    count = count_ref[0]
     for j in range(8):
         rim_ref[j] = jnp.full((PLANES, 8, 128), 0.0 if j < 6 else 1.0, F32)
         rim_ref[j, 1:33, 7, :] = below_ref[CX * j : CX * (j + 1), :]
@@ -552,7 +550,6 @@
         for g, groups in ((0, 1), (11, 1 + REACH)):
             start = DEPTH * part + 128 * g
             ut_ref[:, start : start + 128 * groups] = jnp.zeros((768, 128 * groups), BF16)
-    sorted_ref[...] = jnp.zeros(sorted_ref.shape, F32)
 
     def old(g):
         return lambda j: jnp.stack([own_plane(u_ref, rho_ref, rim_ref, j, 3 * g + i) for i in range(3)])
@@ -568,28 +565,40 @@
     advance(
         pl.ds(30, 3), old(10), grid_ref, fresh_ref, [(0, 29), (1, 30)], ut_ref, 1280, DEPTH, (True, True, False)
     )
-    interpolate(list_ref, span_ref, None, 2 * ((count + 3) // 4), ut_ref, a_ref, wx_ref, sorted_ref)
-
-
-def middle(count, span, markers, u_old, density, below, above, grid):
+
+
+def middle(u_old, density, below, above, grid):
     return pl.pallas_call(
         middle_kernel,
         out_shape=[
             jax.ShapeDtypeStruct((6, CX, CY, 128), F32),
             jax.ShapeDtypeStruct((8, PLANES, 8, 128), F32),
-            jax.ShapeDtypeStruct((8, 128 * TILES + 256), F32),
-        ],
-        in_specs=[SMEM, SMEM] + [VMEM] * 6,
+            jax.ShapeDtypeStruct((768, 2 * DEPTH), BF16),
+        ],
+        in_specs=[VMEM] * 5,
         out_specs=[VMEM] * 3,
         compiler_params=pltpu.CompilerParams(vmem_limit_bytes=24 * MIB),
-        scratch_shapes=[
-            pltpu.VMEM((768, 2 * DEPTH), BF16),
-            pltpu.VMEM((2, 2 * 128 * REACH, 256), BF16),
-            pltpu.VMEM((2, 16, 256), F32),
-        ],
+        cost_estimate=pl.CostEstimate(flops=3_000_000_000, bytes_accessed=6_000_000, transcendentals=0),
+        name="middle",
+    )(u_old, density, below, above, grid)
+
+
+def inner_kernel(count_ref, span_ref, list_ref, ut_ref, sorted_ref, a_ref, wx_ref):
+    sorted_ref[...] = jnp.zeros(sorted_ref.shape, F32)
+    interpolate(list_ref, span_ref, None, 2 * ((count_ref[0] + 3) // 4), ut_ref, a_ref, wx_ref, sorted_ref)
+
+
+def inner(count, span, markers, ut):
+    return pl.pallas_call(
+        inner_kernel,
+        out_shape=jax.ShapeDtypeStruct((8, 128 * TILES + 256), F32),
+        in_specs=[SMEM, SMEM, VMEM, VMEM],
+        out_specs=VMEM,
+        compiler_params=pltpu.CompilerParams(vmem_limit_bytes=24 * MIB),
+        scratch_shapes=[pltpu.VMEM((2, 2 * 128 * REACH, 256), BF16), pltpu.VMEM((2, 16, 256), F32)],
         cost_estimate=pl.CostEstimate(flops=6_000_000_000, bytes_accessed=6_000_000, transcendentals=0),
-        name="middle",
-    )(count, span, markers, u_old, density, below, above, grid)
+        name="inner",
+    )(count, span, markers, ut)
 
 
 def finish_kernel(
@@ -705,10 +714,9 @@
     grid = spread(tile_count, span, markers)
     to_next, to_previous, grid = pack_x(u_old, density, below, above, markers, grid)
     left = shift(to_next, "gx", 1)
+    fresh, rim, ut = middle(u_old, density, below, above, grid)
     right = shift(to_previous, "gx", -1)
-    fresh, rim, sorted_list = middle(
-        tile_count, span, markers, u_old, density, below, above, grid
-    )
+    sorted_list = inner(tile_count, span, markers, ut)
     return finish(
         tile_count, span, markers, pos, u_old, density, rim, left, right, grid, fresh, sorted_list
     )

time: 42.2 us -> 42.2 us (level)
  the two profiles are of different devices: /device:TPU:13 before, /device:TPU:24 now
where the time goes in v5:
time: 42.2 us; the launch traced here: 42.1 us
  Pallas kernels  30.8 us (73%)
  starting transfers between devices  8.76 us (21%)
  between operations  1.56 us (4%)
  local copies, waits for them, and re-layouts  0.92 us (2%)
    ppermute x4, starting transfers between devices, shift(): lax.ppermute(value, axis, [(i, (i + steps) % count) for i in range(count)])  8.76 us
    pallas_call x1, Pallas kernels, spread(): pl.pallas_call(spread_kernel, out_shape=jax.ShapeDtypeStruct((6, PLANES +...  7.44 us
    pallas_call x1, Pallas kernels, inner(): pl.pallas_call(inner_kernel, out_shape=jax.ShapeDtypeStruct((8, 128 * TIL...  6.52 us
    pallas_call x1, Pallas kernels, finish(): pl.pallas_call(finish_kernel, out_shape=[jax.ShapeDtypeStruct(u_old.shape...  5.57 us
    pallas_call x1, Pallas kernels, pack_y(): pl.pallas_call(pack_y_kernel, out_shape=[jax.ShapeDtypeStruct((8 * CX + L...  3.63 us
    pallas_call x1, Pallas kernels, sort(): pl.pallas_call(sort_kernel, out_shape=[jax.ShapeDtypeStruct((LIST, 128),...  3.18 us
    pallas_call x1, Pallas kernels, middle(): pl.pallas_call(middle_kernel, out_shape=[jax.ShapeDtypeStruct((6, CX, CY,...  2.95 us
    pallas_call x1, Pallas kernels, pack_x(): pl.pallas_call(pack_x_kernel, out_shape=[jax.ShapeDtypeStruct((8 * ROWS +...  1.52 us
  transfers between devices with their start and end apart: 4, of which 0 were waited for; matrix products, arithmetic and copies ran while one was open for 0% of the time, Pallas kernels for 48%

profile of v5, /device:TPU:24, one launch (start us, length us, event | category | flops | bytes accessed | tf_op | source)
XLA Modules:
  0.0 42.1 jit_solution(3551151106148303277)
XLA Ops:
  1.3 3.6 %pack_y.1 = (f32[408,128]{1,0:T(8,128)}, f32[664,128]{1,0:T(8,128)}, f32[16,2048]{1,0:T(8,128)}) custom-call(s32[1]{0:T(128)S(6)} %copy.18.count_ref, f32[3,16,128]{2,1,0:T(8,128)} %off_hbm.1, f32[3,16,128]{2,1,0:T(8,128)} %force_hbm.1, s32[16,128]{1,0:T(8,128)} %bx_hbm.1, s32[16,128]{1,0:T(8,128)} %by_hbm.1, s32[16,128]{1,0:T(8,128)} %bz_hbm.1, ...), custom_call_target="tpu_custom_call" | custom-call | tf_op jit(solution)/shard_map/pack_y/pallas_call | solution.py:199
  4.9 2.0 %collective-permute-start = (f32[408,128]{1,0:T(8,128)}, f32[408,128]{1,0:T(8,128)S(1)}, u32[]{:S(2)}, u32[]{:S(2)}) collective-permute-start(f32[408,128]{1,0:T(8,128)} %get-tuple-element.20), channel_id=1, source_target_pairs={{0,1},{1,2},{2,3},{3,4},{4,5},{5,6},{6,7},{7,8},{8,9},{9,10},{10,1... | collective-permute-start | bytes 626696 | tf_op jit(solution)/shard_map/ppermute | solution.py:705
  6.9 5.0 %collective-permute-start.1 = (f32[664,128]{1,0:T(8,128)}, f32[664,128]{1,0:T(8,128)S(1)}, u32[]{:S(2)}, u32[]{:S(2)}) collective-permute-start(f32[664,128]{1,0:T(8,128)} %get-tuple-element.21), channel_id=1, source_target_pairs={{0,15},{1,0},{2,1},{3,2},{4,3},{5,4},{6,5},{7,6},{8,7},{9,8},{10,9... | collective-permute-start | bytes 1019912 | tf_op jit(solution)/shard_map/ppermute | solution.py:705
  11.9 0.0 copy-start.2
  11.9 0.9 %copy-done.2 = f32[16,2048]{1,0:T(8,128)S(1)} copy-done((f32[16,2048]{1,0:T(8,128)S(1)}, f32[16,2048]{1,0:T(8,128)}, u32[]{:S(2)}) %copy-start.2) | copy-done | bytes 131096
  12.8 3.2 %sort.1 = (f32[152,128]{1,0:T(8,128)S(1)}, f32[16,128]{1,0:T(8,128)S(1)}, s32[16]{0:T(128)S(1)}) custom-call(s32[1]{0:T(128)S(6)} %copy.18.count_ref, f32[16,2048]{1,0:T(8,128)S(1)} %copy-done.2), custom_call_target="tpu_custom_call" | custom-call | flops 3000000000 | bytes 400000 | tf_op jit(solution)/shard_map/sort/pallas_call | solution.py:256
  16.0 0.0 copy-start
  16.0 0.0 copy-start.1
  16.0 7.4 %spread.1.grid_in = f32[6,45,40,128]{3,2,1,0:T(8,128)S(1)} custom-call(s32[1]{0:T(128)S(6)} %copy.18.count_ref, s32[16]{0:T(128)S(1)} %get-tuple-element.17.span_ref, f32[152,128]{1,0:T(8,128)S(1)} %get-tuple-element.18.list_ref), custom_call_target="tpu_custom_call" | custom-call | flops 6000000000 | bytes 6000000 | tf_op jit(solution)/shard_map/spread/pallas_call | solution.py:377
  23.4 0.0 collective-permute-done.below_ref
  23.4 0.0 collective-permute-done.1.above_ref
  23.5 0.0 copy-done
  23.5 0.0 copy-done.1
  23.5 1.5 %pack_x.1 = (f32[616,128]{1,0:T(8,128)S(1)}, f32[936,128]{1,0:T(8,128)S(1)}, f32[6,45,40,128]{3,2,1,0:T(8,128)S(1)}) custom-call(f32[3,32,32,256]{3,2,1,0:T(8,128)S(1)} %copy-done, f32[32,32,256]{2,1,0:T(8,128)S(1)} %copy-done.1, f32[408,128]{1,0:T(8,128)S(1)} %collective-permute-done.below_ref, ...), custom_call_target="tpu_custom_call", output_to_operand_aliasing={{2}: (5, {})} | custom-call | tf_op jit(solution)/shard_map/pack_x/pallas_call | solution.py:433
  25.0 0.1 collective-permute-start.2
  25.1 1.7 %collective-permute-start.3 = (f32[936,128]{1,0:T(8,128)S(1)}, f32[936,128]{1,0:T(8,128)S(1)}, u32[]{:S(2)}, u32[]{:S(2)}) collective-permute-start(f32[936,128]{1,0:T(8,128)S(1)} %get-tuple-element.25), channel_id=1, source_target_pairs={{0,240},{16,0},{32,16},{48,32},{64,48},{80,64},{96,80},{112,96},{1... | collective-permute-start | bytes 1437704 | tf_op jit(solution)/shard_map/ppermute | solution.py:705
  26.8 3.0 %middle.1 = (f32[6,32,32,128]{3,2,1,0:T(8,128)S(1)}, f32[8,36,8,128]{3,2,1,0:T(8,128)S(1)}, bf16[768,4096]{1,0:T(8,128)(2,1)S(1)}) custom-call(f32[3,32,32,256]{3,2,1,0:T(8,128)S(1)} %copy-done, f32[32,32,256]{2,1,0:T(8,128)S(1)} %copy-done.1, f32[408,128]{1,0:T(8,128)S(1)} %collective-permute-done.below_ref, ...), custom_call_target="tpu_custom_call" | custom-call | flops 3000000000 | bytes 6000000 | tf_op jit(solution)/shard_map/middle/pallas_call | solution.py:571
  29.8 6.5 %inner.1.sorted_in = f32[8,2304]{1,0:T(8,128)S(1)} custom-call(s32[1]{0:T(128)S(6)} %copy.18.count_ref, s32[16]{0:T(128)S(1)} %get-tuple-element.17.span_ref, f32[152,128]{1,0:T(8,128)S(1)} %get-tuple-element.18.list_ref, bf16[768,4096]{1,0:T(8,128)(2,1)S(1)} %get-tuple-element.27.ut_ref), custom_call_target="tpu_custom_call" | custom-call | flops 6000000000 | bytes 6000000 | tf_op jit(solution)/shard_map/inner/pallas_call | solution.py:592
  36.3 0.0 collective-permute-done.2.left_ref
  36.3 0.0 collective-permute-done.3.right_ref
  36.3 5.6 %finish.1 = (f32[3,32,32,256]{3,2,1,0:T(8,128)}, f32[3,16,128]{2,1,0:T(8,128)}, f32[6,45,40,128]{3,2,1,0:T(8,128)S(1)}, f32[6,32,32,128]{3,2,1,0:T(8,128)S(1)}, f32[8,2304]{1,0:T(8,128)S(1)}) custom-call(s32[1]{0:T(128)S(6)} %copy.18.count_ref, s32[16]{0:T(128)S(1)} %get-tuple-element.17.span_ref, ...), custom_call_target="tpu_custom_call", output_to_operand_aliasing={{2}: (9, {}), {3}: (10, {}), {4}: (11, {})} | custom-call | flops 6000000000 | bytes 12000000 | tf_op jit(solution)/shard_map/finish/pallas_call | solution.py:678
Async XLA Ops:
  4.9 18.5 %collective-permute-start = (f32[408,128]{1,0:T(8,128)}, f32[408,128]{1,0:T(8,128)S(1)}, u32[]{:S(2)}, u32[]{:S(2)}) collective-permute-start(f32[408,128]{1,0:T(8,128)} %get-tuple-element.20), channel_id=1, source_target_pairs={{0,1},{1,2},{2,3},{3,4},{4,5},{5,6},{6,7},{7,8},{8,9},{9,10},{10,1... | collective-permute-start | bytes 626696 | tf_op jit(solution)/shard_map/ppermute | solution.py:705
  6.9 16.5 %collective-permute-start.1 = (f32[664,128]{1,0:T(8,128)}, f32[664,128]{1,0:T(8,128)S(1)}, u32[]{:S(2)}, u32[]{:S(2)}) collective-permute-start(f32[664,128]{1,0:T(8,128)} %get-tuple-element.21), channel_id=1, source_target_pairs={{0,15},{1,0},{2,1},{3,2},{4,3},{5,4},{6,5},{7,6},{8,7},{9,8},{10,9... | collective-permute-start | bytes 1019912 | tf_op jit(solution)/shard_map/ppermute | solution.py:705
  11.9 0.9 %copy-start.2 = (f32[16,2048]{1,0:T(8,128)S(1)}, f32[16,2048]{1,0:T(8,128)}, u32[]{:S(2)}) copy-start(f32[16,2048]{1,0:T(8,128)} %get-tuple-element.16.pay_ref) | copy-start | bytes 393220
  16.0 7.5 %copy-start = (f32[3,32,32,256]{3,2,1,0:T(8,128)S(1)}, f32[3,32,32,256]{3,2,1,0:T(8,128)}, u32[]{:S(2)}) copy-start(f32[3,32,32,256]{3,2,1,0:T(8,128)} %u_ref.7) | copy-start | bytes 9437188
  16.0 7.5 %copy-start.1 = (f32[32,32,256]{2,1,0:T(8,128)S(1)}, f32[32,32,256]{2,1,0:T(8,128)}, u32[]{:S(2)}) copy-start(f32[32,32,256]{2,1,0:T(8,128)} %rho_ref.7) | copy-start | bytes 3145732
  25.0 11.3 %collective-permute-start.2 = (f32[616,128]{1,0:T(8,128)S(1)}, f32[616,128]{1,0:T(8,128)S(1)}, u32[]{:S(2)}, u32[]{:S(2)}) collective-permute-start(f32[616,128]{1,0:T(8,128)S(1)} %get-tuple-element.24), channel_id=1, source_target_pairs={{0,16},{16,32},{32,48},{48,64},{64,80},{80,96},{96,112},{112,128},... | collective-permute-start | bytes 946184 | tf_op jit(solution)/shard_map/ppermute | solution.py:705
  25.1 11.2 %collective-permute-start.3 = (f32[936,128]{1,0:T(8,128)S(1)}, f32[936,128]{1,0:T(8,128)S(1)}, u32[]{:S(2)}, u32[]{:S(2)}) collective-permute-start(f32[936,128]{1,0:T(8,128)S(1)} %get-tuple-element.25), channel_id=1, source_target_pairs={{0,240},{16,0},{32,16},{48,32},{64,48},{80,64},{96,80},{112,96},{1... | collective-permute-start | bytes 1437704 | tf_op jit(solution)/shard_map/ppermute | solution.py:705
